TPU v7x, 512 devices: a whole 4x4x16 slice. The times are simulated.
512 devices in a mesh: row: 16 (over z), col: 16 (over y, x), layer: 2 (over core).
Axes of the slice: x: 4, y: 4, z: 16, core: 2. Of those that a mesh axis runs over, the one named last changes fastest.
Arguments:
- ratings: bfloat16 [32768, 16384], P('row', ('col', 'layer')), may hold values from -6 to 6
- tile_mask: int32 [256, 128], P('row', ('col', 'layer')), may hold values 0 or 1
- tile_counts: int32 [256, 128], P('row', ('col', 'layer')), may hold values from 1 to 16384
- user_factor: float32 [256, 32768], P(('col', 'layer'), 'row'), may hold values from -1.5 to 1.5
- item_factor: float32 [256, 16384], P('row', ('col', 'layer')), may hold values from -1.5 to 1.5
Outputs:
- new_user: float32 [256, 32768], P(('col', 'layer'), 'row')
- new_item: float32 [256, 16384], P('row', ('col', 'layer'))
- loss_value: float32 [], replicated
- grad_norm: float32 [], replicated
All inputs are finite; a program needn't handle non-finite values. No bound on the sum of `tile_mask` on one device may be relied on, other than what follows from the above.
Results may differ from a plain program's by a relative error of at most 0.0049.
Values may be sent and summed in bfloat16 or wider, within the bound.
No kernel may reach another device: no remote copies, remote signals or barrier semaphores. Data moves between devices by JAX's collectives and lax.ppermute only.
A program may use at most 64 MiB of HBM per device.

v0:
```python
import jax
import jax.numpy as jnp
from jax import lax
from jax.sharding import Mesh
from jax.sharding import PartitionSpec as P

TILE = 128
COL_LAYER = ("col_0", "col_1", "layer")
ROW_COL_LAYER = ("row", "col_0", "col_1", "layer")


epsilon = 1e-12
trust_ratio = 0.2


def from_everyone(array, axis):
    count = lax.axis_size(axis)
    return lax.all_to_all(
        jnp.broadcast_to(array[None], (count, *array.shape)), axis, 0, 0, tiled=True
    )


def joined_along(blocks, dim):
    dims = list(blocks.shape[1:])
    dims[dim] *= blocks.shape[0]
    return jnp.moveaxis(blocks, 0, dim).reshape(dims)


def gather_directly(array, axis, dim):
    blocks = from_everyone(array, axis)
    return joined_along(blocks, dim)


def by_axis(array, axes):
    for axis in axes:
        array = lax.psum(array, axis)
    return array


def in_blocks(array, dim, count):
    dims = array.shape
    blocks = array.reshape(*dims[:dim], count, dims[dim] // count, *dims[dim + 1 :])
    return jnp.moveaxis(blocks, dim, 0)


def sent_and_summed(array, axis, dim):
    blocks = in_blocks(array, dim, lax.axis_size(axis))
    arrived = lax.all_to_all(blocks, axis, split_axis=0, concat_axis=0, tiled=True)
    return arrived.astype(jnp.float32).sum(axis=0)


def tile_weights(mask_rows, count_rows):
    side = TILE
    position = lax.broadcasted_iota(jnp.int32, (side, side), 0) * side + lax.broadcasted_iota(
        jnp.int32, (side, side), 1
    )
    observed = (mask_rows[:, None, :, None] == 1) & (
        position[None, :, None, :] < count_rows[:, None, :, None]
    )
    return observed.astype(jnp.float32).reshape(
        mask_rows.shape[0] * side, mask_rows.shape[1] * side
    )


def body(ratings, tile_mask, tile_counts, user_factor, item_factor):
    user_low = user_factor.astype(jnp.bfloat16)
    item_low = item_factor.astype(jnp.bfloat16)
    user_rows = gather_directly(user_low, COL_LAYER, 0)
    item_cols = gather_directly(item_low, "row", 0)
    count_local = jnp.sum(tile_mask * tile_counts).astype(jnp.float32)
    factor_local = jnp.sum(user_factor * user_factor) + jnp.sum(item_factor * item_factor)
    predicted = lax.dot_general(
        user_rows, item_cols, (((0,), (0,)), ((), ())), preferred_element_type=jnp.float32
    )
    residual = tile_weights(tile_mask, tile_counts) * (predicted - ratings.astype(jnp.float32))
    scaled = residual.astype(jnp.bfloat16)
    error_local = jnp.sum(residual * residual)
    count_sum, factor_sum, error_sum = (
        by_axis(count_local, ROW_COL_LAYER),
        by_axis(factor_local, ROW_COL_LAYER),
        by_axis(error_local, ROW_COL_LAYER),
    )
    factor_part = user_rows
    raw_item = sent_and_summed(
        jnp.dot(factor_part, scaled, preferred_element_type=jnp.float32).astype(jnp.bfloat16),
        "row",
        0,
    )
    factor_part = item_cols
    raw_user = sent_and_summed(
        lax.dot_general(
            factor_part, scaled, (((1,), (1,)), ((), ())), preferred_element_type=jnp.float32
        ).astype(jnp.bfloat16),
        COL_LAYER,
        0,
    )
    gradient_local = jnp.sum(raw_user * raw_user) + jnp.sum(raw_item * raw_item)
    gradient_sum = by_axis(gradient_local, ROW_COL_LAYER)
    observed_total = jnp.maximum(count_sum, jnp.float32(1.0))
    loss_value = error_sum / observed_total
    grad_norm = 2.0 / observed_total * jnp.sqrt(gradient_sum + epsilon)
    factor_norm = jnp.sqrt(factor_sum + epsilon)
    rate = trust_ratio * factor_norm / grad_norm
    step_size = rate * (2.0 / observed_total)
    new_user = user_factor - step_size * raw_user
    new_item = item_factor - step_size * raw_item
    return (new_user, new_item, loss_value, grad_norm)


def solution(mesh):
    finer = Mesh(
        mesh.devices.reshape(mesh.shape["row"], 4, 4, mesh.shape["layer"]),
        ("row", "col_0", "col_1", "layer"),
    )
    return jax.shard_map(
        body,
        mesh=finer,
        in_specs=(
            P("row", COL_LAYER),
            P("row", COL_LAYER),
            P("row", COL_LAYER),
            P(COL_LAYER, "row"),
            P("row", COL_LAYER),
        ),
        out_specs=(P(COL_LAYER, "row"), P("row", COL_LAYER), P(), P()),
        check_vma=False,
    )
```

profile of v0, /device:TPU:1, one launch (start us, length us, event | category | flops | bytes accessed | tf_op | source)
XLA Modules:
  0.0 176.2 jit_solution(6132000480755298234)
XLA Ops:
  0.6 0.0 copy-start.3
  0.6 0.0 copy-start.2
  0.7 1.4 multiply_reduce_fusion.4
  2.1 0.7 broadcast_in_dim.5
  2.8 15.7 %all-to-all-start.1 = ((bf16[16,16,512]{2,1,0:T(8,128)(2,1)}), bf16[16,16,512]{2,1,0:T(8,128)(2,1)S(1)}, u32[]{:S(2)}, u32[]{:S(2)}) async-start(bf16[16,16,512]{2,1,0:T(8,128)(2,1)} %broadcast_in_dim.5), calls=%async_computation.1 | async-start | bytes 524288 | tf_op jit(solution)/shard_map/all_to_all | solution.py:18
  18.6 1.5 multiply_reduce_fusion.2
  20.1 12.2 %all-to-all-done.1 = bf16[16,16,512]{2,1,0:T(8,128)(2,1)S(1)} async-done(((bf16[16,16,512]{2,1,0:T(8,128)(2,1)}), bf16[16,16,512]{2,1,0:T(8,128)(2,1)S(1)}, u32[]{:S(2)}, u32[]{:S(2)}) %all-to-all-start.1) | async-done | bytes 262176 | tf_op jit(solution)/shard_map/all_to_all | solution.py:18
  32.3 1.1 broadcast_in_dim.4
  33.4 12.6 %all-to-all-start = ((bf16[32,8,2048]{2,1,0:T(8,128)(2,1)}), bf16[32,8,2048]{2,1,0:T(8,128)(2,1)S(1)}, u32[]{:S(2)}, u32[]{:S(2)}) async-start(bf16[32,8,2048]{2,1,0:T(8,128)(2,1)} %broadcast_in_dim.4), calls=%async_computation | async-start | bytes 2097152 | tf_op jit(solution)/shard_map/all_to_all | solution.py:18
  46.1 0.0 copy-done.3
  46.1 0.1 copy.9
  46.2 0.0 copy-done.2
  46.2 0.1 copy.10
  46.3 0.1 iota_add_fusion
  46.4 1.4 compare_and_fusion
  47.9 15.3 %all-to-all-done = bf16[32,8,2048]{2,1,0:T(8,128)(2,1)S(1)} async-done(((bf16[32,8,2048]{2,1,0:T(8,128)(2,1)}), bf16[32,8,2048]{2,1,0:T(8,128)(2,1)S(1)}, u32[]{:S(2)}, u32[]{:S(2)}) %all-to-all-start) | async-done | bytes 1048608 | tf_op jit(solution)/shard_map/all_to_all | solution.py:18
  63.1 4.1 %multiply_reduce_fusion = (f32[]{:T(128)}, bf16[2048,512]{1,0:T(8,128)(2,1)S(1)}) fusion(bf16[2048,512]{1,0:T(8,128)(2,1)} %param.5, bf16[256,512]{1,0:T(8,128)(2,1)S(1)} %bitcast.24, bf16[32,8,2048]{2,1,0:T(8,128)(2,1)S(1)} %all-to-all-done, pred[256,8,4,128]{3,2,1,0:T(4,128)(4,1)S(1)} %bitcast.23), kind=kOutput, calls=%fused_computation | convolution fusion | flops 543162368 | bytes 6553604 | tf_op jit(solution)/shard_map/dot_general | solution.py:72
  67.3 0.0 copy-start.4
  67.3 1.4 convolution_convert_fusion.1
  68.7 0.0 copy-done.4
  68.7 5.5 %all-to-all-start.3 = ((bf16[16,16,512]{2,1,0:T(8,128)(2,1)}), bf16[16,16,512]{2,1,0:T(8,128)(2,1)S(1)}, u32[]{:S(2)}, u32[]{:S(2)}) async-start(bf16[16,16,512]{2,1,0:T(8,128)(2,1)} %bitcast.5), calls=%async_computation.3 | async-start | bytes 524288 | tf_op jit(solution)/shard_map/all_to_all | solution.py:48
  74.2 3.3 %fusion = bf16[32,8,2048]{2,1,0:T(8,128)(2,1)} fusion(bf16[256,512]{1,0:T(8,128)(2,1)S(1)} %bitcast.25, bf16[2048,512]{1,0:T(8,128)(2,1)} %copy-done.4), kind=kOutput, calls=%fused_computation.4 | convolution fusion | flops 537395200 | bytes 3407872 | tf_op jit(solution)/shard_map/dot_general | solution.py:91
  77.5 0.0 copy-start.1
  77.5 0.0 copy-start
  77.5 10.7 %all-to-all-done.3 = bf16[16,16,512]{2,1,0:T(8,128)(2,1)S(1)} async-done(((bf16[16,16,512]{2,1,0:T(8,128)(2,1)}), bf16[16,16,512]{2,1,0:T(8,128)(2,1)S(1)}, u32[]{:S(2)}, u32[]{:S(2)}) %all-to-all-start.3) | async-done | bytes 262176 | tf_op jit(solution)/shard_map/all_to_all | solution.py:48
  88.2 8.8 %all-to-all-start.2 = ((bf16[32,8,2048]{2,1,0:T(8,128)(2,1)}), bf16[32,8,2048]{2,1,0:T(8,128)(2,1)S(1)}, u32[]{:S(2)}, u32[]{:S(2)}) async-start(bf16[32,8,2048]{2,1,0:T(8,128)(2,1)} %fusion), calls=%async_computation.2 | async-start | bytes 2097152 | tf_op jit(solution)/shard_map/all_to_all | solution.py:48
  97.0 0.6 multiply_reduce_fusion.5
  99.6 0.6 multiply_reduce_fusion.3
  100.2 13.9 %all-to-all-done.2 = bf16[32,8,2048]{2,1,0:T(8,128)(2,1)S(1)} async-done(((bf16[32,8,2048]{2,1,0:T(8,128)(2,1)}), bf16[32,8,2048]{2,1,0:T(8,128)(2,1)S(1)}, u32[]{:S(2)}, u32[]{:S(2)}) %all-to-all-start.2) | async-done | bytes 1048608 | tf_op jit(solution)/shard_map/all_to_all | solution.py:48
  114.1 0.2 convert_reduce_fusion
  114.2 0.6 multiply_reduce_fusion.1
  116.2 24.6 %all-reduce = (f32[]{:T(128)}, f32[]{:T(128)}, f32[]{:T(128)}, f32[]{:T(128)}) all-reduce(f32[]{:T(128)S(6)} %add.51, f32[]{:T(128)S(6)} %convert_element_type.35, f32[]{:T(128)S(6)} %add.54, f32[]{:T(128)} %get-tuple-element.24), channel_id=1, replica_groups=mesh['row'=16,'col_0'=4,'col_1'=4,'layer'=2] {'row'}, use_global_device_ids=true, to_apply=%region_2.0 | all-reduce | flops 4 | bytes 32 | tf_op jit(solution)/shard_map/psum | solution.py:36
  140.8 7.1 %all-reduce.2 = (f32[]{:T(128)}, f32[]{:T(128)}, f32[]{:T(128)}, f32[]{:T(128)}) all-reduce(f32[]{:T(128)} %get-tuple-element.4, f32[]{:T(128)} %get-tuple-element.5, f32[]{:T(128)} %get-tuple-element.6, f32[]{:T(128)} %get-tuple-element.7), channel_id=1, replica_groups=mesh['row'=16,'col_0'=4,'col_1'=4,'layer'=2] {'col_0'}, use_global_device_ids=true, to_apply=%region_3.0 | all-reduce | flops 4 | bytes 32 | tf_op jit(solution)/shard_map/psum | solution.py:36
  147.9 8.6 %all-reduce.1 = (f32[]{:T(128)}, f32[]{:T(128)}, f32[]{:T(128)}, f32[]{:T(128)}) all-reduce(f32[]{:T(128)} %get-tuple-element.12, f32[]{:T(128)} %get-tuple-element.13, f32[]{:T(128)} %get-tuple-element.14, f32[]{:T(128)} %get-tuple-element.15), channel_id=1, replica_groups=mesh['row'=16,'col_0'=4,'col_1'=4,'layer'=2] {'col_1'}, use_global_device_ids=true, to_apply=%region_4.0 | all-reduce | flops 4 | bytes 32 | tf_op jit(solution)/shard_map/psum | solution.py:36
  156.5 13.3 %all-reduce.3 = (f32[]{:T(128)}, f32[]{:T(128)}, f32[]{:T(128)}, f32[]{:T(128)}) all-reduce(f32[]{:T(128)} %get-tuple-element.8, f32[]{:T(128)} %get-tuple-element.9, f32[]{:T(128)} %get-tuple-element.10, f32[]{:T(128)} %get-tuple-element.11), channel_id=1, replica_groups=mesh['row'=16,'col_0'=4,'col_1'=4,'layer'=2] {'layer'}, use_global_device_ids=true, to_apply=%region_5.0 | all-reduce | flops 4 | bytes 32 | tf_op jit(solution)/shard_map/psum | solution.py:36
  171.9 0.0 copy-done.1
  171.9 0.6 multiply_subtract_fusion.1
  172.6 0.0 copy-done
  172.6 0.6 multiply_subtract_fusion
  (3 shorter events, 0.1 us)
Async XLA Ops:
  0.6 45.5 %copy-start.3 = (s32[16,4]{0,1:T(4,128)S(1)}, s32[16,4]{0,1:T(4,128)}, u32[]{:S(2)}) copy-start(s32[16,4]{0,1:T(4,128)} %param.6) | copy-start | bytes 772
  0.6 45.6 %copy-start.2 = (s32[16,4]{0,1:T(4,128)S(1)}, s32[16,4]{0,1:T(4,128)}, u32[]{:S(2)}) copy-start(s32[16,4]{0,1:T(4,128)} %param.7) | copy-start | bytes 772
  2.8 29.5 %all-to-all-start.1 = ((bf16[16,16,512]{2,1,0:T(8,128)(2,1)}), bf16[16,16,512]{2,1,0:T(8,128)(2,1)S(1)}, u32[]{:S(2)}, u32[]{:S(2)}) async-start(bf16[16,16,512]{2,1,0:T(8,128)(2,1)} %broadcast_in_dim.5), calls=%async_computation.1 | async-start | bytes 524288 | tf_op jit(solution)/shard_map/all_to_all | solution.py:18
  33.4 29.7 %all-to-all-start = ((bf16[32,8,2048]{2,1,0:T(8,128)(2,1)}), bf16[32,8,2048]{2,1,0:T(8,128)(2,1)S(1)}, u32[]{:S(2)}, u32[]{:S(2)}) async-start(bf16[32,8,2048]{2,1,0:T(8,128)(2,1)} %broadcast_in_dim.4), calls=%async_computation | async-start | bytes 2097152 | tf_op jit(solution)/shard_map/all_to_all | solution.py:18
  67.3 1.4 copy-start.4
  68.7 19.5 %all-to-all-start.3 = ((bf16[16,16,512]{2,1,0:T(8,128)(2,1)}), bf16[16,16,512]{2,1,0:T(8,128)(2,1)S(1)}, u32[]{:S(2)}, u32[]{:S(2)}) async-start(bf16[16,16,512]{2,1,0:T(8,128)(2,1)} %bitcast.5), calls=%async_computation.3 | async-start | bytes 524288 | tf_op jit(solution)/shard_map/all_to_all | solution.py:48
  77.5 94.4 %copy-start.1 = (f32[16,512]{1,0:T(8,128)S(1)}, f32[16,512]{1,0:T(8,128)}, u32[]{:S(2)}) copy-start(f32[16,512]{1,0:T(8,128)} %param.9) | copy-start | bytes 98308
  77.5 95.0 %copy-start = (f32[8,2048]{1,0:T(8,128)S(1)}, f32[8,2048]{1,0:T(8,128)}, u32[]{:S(2)}) copy-start(f32[8,2048]{1,0:T(8,128)} %param.8) | copy-start | bytes 196612
  88.2 25.9 %all-to-all-start.2 = ((bf16[32,8,2048]{2,1,0:T(8,128)(2,1)}), bf16[32,8,2048]{2,1,0:T(8,128)(2,1)S(1)}, u32[]{:S(2)}, u32[]{:S(2)}) async-start(bf16[32,8,2048]{2,1,0:T(8,128)(2,1)} %fusion), calls=%async_computation.2 | async-start | bytes 2097152 | tf_op jit(solution)/shard_map/all_to_all | solution.py:48
where the time goes:
time: 177 us; the launch traced here: 176 us
  blocking collectives  53.6 us (30%)
  waiting for transfers between devices  52.1 us (29%)
  starting transfers between devices  42.6 us (24%)
  between operations  9.06 us (5%)
  matrix products  8.87 us (5%)
  other arithmetic  7.83 us (4%)
  local copies, waits for them, and re-layouts  2.03 us (1%)
    psum x4, blocking collectives, by_axis(): array = lax.psum(array, axis)  53.6 us
    all_to_all x2, starting transfers between devices, from_everyone(): lax.all_to_all(jnp.broadcast_to(array[None], (count, *array.shape)), axis...  28.4 us
    all_to_all x2, waiting for transfers between devices, from_everyone(): lax.all_to_all(jnp.broadcast_to(array[None], (count, *array.shape)), axis...  27.5 us
    all_to_all x2, waiting for transfers between devices, sent_and_summed(): lax.all_to_all(blocks, axis, split_axis=0, concat_axis=0, tiled=True)  24.5 us
    all_to_all x2, starting transfers between devices, sent_and_summed(): lax.all_to_all(blocks, axis, split_axis=0, concat_axis=0, tiled=True)  14.3 us
    dot_general x1, matrix products, body(): lax.dot_general(user_rows, item_cols, (((0,), (0,)), ((), ())), preferred...  4.12 us
  transfers between devices with their start and end apart: 4, of which 4 were waited for; matrix products, arithmetic and copies ran while one was open for 4% of the time, Pallas kernels for 0%

commit v1 on v0

--- a/solution.py
+++ b/solution.py
@@ -6,7 +6,6 @@
 
 TILE = 128
 COL_LAYER = ("col_0", "col_1", "layer")
-ROW_COL_LAYER = ("row", "col_0", "col_1", "layer")
 
 
 epsilon = 1e-12
@@ -31,21 +30,18 @@
     return joined_along(blocks, dim)
 
 
-def by_axis(array, axes):
-    for axis in axes:
-        array = lax.psum(array, axis)
-    return array
-
-
 def in_blocks(array, dim, count):
     dims = array.shape
     blocks = array.reshape(*dims[:dim], count, dims[dim] // count, *dims[dim + 1 :])
     return jnp.moveaxis(blocks, dim, 0)
 
 
-def sent_and_summed(array, axis, dim):
+def sent(array, axis, dim):
     blocks = in_blocks(array, dim, lax.axis_size(axis))
-    arrived = lax.all_to_all(blocks, axis, split_axis=0, concat_axis=0, tiled=True)
+    return lax.all_to_all(blocks, axis, split_axis=0, concat_axis=0, tiled=True)
+
+
+def summed(arrived):
     return arrived.astype(jnp.float32).sum(axis=0)
 
 
@@ -62,11 +58,18 @@
     )
 
 
+def scalars_summed(scalars):
+    packed = jnp.stack(scalars + [jnp.float32(0.0)] * (TILE - len(scalars)))[None]
+    packed = from_everyone(packed, COL_LAYER).sum(axis=0)
+    packed = from_everyone(packed, "row").sum(axis=0)
+    return [packed[0, i] for i in range(len(scalars))]
+
+
 def body(ratings, tile_mask, tile_counts, user_factor, item_factor):
     user_low = user_factor.astype(jnp.bfloat16)
     item_low = item_factor.astype(jnp.bfloat16)
+    item_cols = gather_directly(item_low, "row", 0)
     user_rows = gather_directly(user_low, COL_LAYER, 0)
-    item_cols = gather_directly(item_low, "row", 0)
     count_local = jnp.sum(tile_mask * tile_counts).astype(jnp.float32)
     factor_local = jnp.sum(user_factor * user_factor) + jnp.sum(item_factor * item_factor)
     predicted = lax.dot_general(
@@ -75,27 +78,18 @@
     residual = tile_weights(tile_mask, tile_counts) * (predicted - ratings.astype(jnp.float32))
     scaled = residual.astype(jnp.bfloat16)
     error_local = jnp.sum(residual * residual)
-    count_sum, factor_sum, error_sum = (
-        by_axis(count_local, ROW_COL_LAYER),
-        by_axis(factor_local, ROW_COL_LAYER),
-        by_axis(error_local, ROW_COL_LAYER),
+    item_share = jnp.dot(user_rows, scaled, preferred_element_type=jnp.float32)
+    item_arrived = sent(item_share.astype(jnp.bfloat16), "row", 0)
+    user_share = lax.dot_general(
+        item_cols, scaled, (((1,), (1,)), ((), ())), preferred_element_type=jnp.float32
     )
-    factor_part = user_rows
-    raw_item = sent_and_summed(
-        jnp.dot(factor_part, scaled, preferred_element_type=jnp.float32).astype(jnp.bfloat16),
-        "row",
-        0,
+    user_arrived = sent(user_share.astype(jnp.bfloat16), COL_LAYER, 0)
+    raw_item = summed(item_arrived)
+    raw_user = summed(user_arrived)
+    gradient_local = jnp.sum(raw_user * raw_user) + jnp.sum(raw_item * raw_item)
+    count_sum, factor_sum, error_sum, gradient_sum = scalars_summed(
+        [count_local, factor_local, error_local, gradient_local]
     )
-    factor_part = item_cols
-    raw_user = sent_and_summed(
-        lax.dot_general(
-            factor_part, scaled, (((1,), (1,)), ((), ())), preferred_element_type=jnp.float32
-        ).astype(jnp.bfloat16),
-        COL_LAYER,
-        0,
-    )
-    gradient_local = jnp.sum(raw_user * raw_user) + jnp.sum(raw_item * raw_item)
-    gradient_sum = by_axis(gradient_local, ROW_COL_LAYER)
     observed_total = jnp.maximum(count_sum, jnp.float32(1.0))
     loss_value = error_sum / observed_total
     grad_norm = 2.0 / observed_total * jnp.sqrt(gradient_sum + epsilon)

time: 177 us -> 152 us (0.86)
  blocking collectives: 53.6 us -> 27.4 us
  local copies, waits for them, and re-layouts: 2.03 us -> 4.06 us
    psum x4 -> x0, blocking collectives: 53.6 us -> none  [by_axis(): array = lax.psum(array, axis)]
    all_to_all x0 -> x2, blocking collectives: none -> 27.4 us  [from_everyone(): lax.all_to_all(jnp.broadcast_to(array[None], (count, *array.shape)), axis...]
  transfers between devices with their start and end apart: 4 -> 4, of which waited for: 4 -> 4; matrix products, arithmetic and copies ran while one was open for 4% -> 6% of each run, Pallas kernels for 0% -> 0%
where the time goes in v1:
time: 152 us; the launch traced here: 151 us
  waiting for transfers between devices  51.4 us (34%)
  starting transfers between devices  42.6 us (28%)
  blocking collectives  27.4 us (18%)
  between operations  9.06 us (6%)
  matrix products  8.94 us (6%)
  other arithmetic  7.87 us (5%)
  local copies, waits for them, and re-layouts  4.06 us (3%)
    all_to_all x2, starting transfers between devices, from_everyone(): lax.all_to_all(jnp.broadcast_to(array[None], (count, *array.shape)), axis...  28.4 us
    all_to_all x2, blocking collectives, from_everyone(): lax.all_to_all(jnp.broadcast_to(array[None], (count, *array.shape)), axis...  27.4 us
    all_to_all x2, waiting for transfers between devices, from_everyone(): lax.all_to_all(jnp.broadcast_to(array[None], (count, *array.shape)), axis...  26.9 us
    all_to_all x2, waiting for transfers between devices, sent(): return lax.all_to_all(blocks, axis, split_axis=0, concat_axis=0, tiled=True)  24.5 us
    all_to_all x2, starting transfers between devices, sent(): return lax.all_to_all(blocks, axis, split_axis=0, concat_axis=0, tiled=True)  14.3 us
    dot_general x1, matrix products, body(): lax.dot_general(user_rows, item_cols, (((0,), (0,)), ((), ())), preferred...  4.13 us
    dot_general x1, matrix products, body(): lax.dot_general(item_cols, scaled, (((1,), (1,)), ((), ())), preferred_el...  3.35 us
  transfers between devices with their start and end apart: 4, of which 4 were waited for; matrix products, arithmetic and copies ran while one was open for 6% of the time, Pallas kernels for 0%

profile of v1, /device:TPU:1, one launch (start us, length us, event | category | flops | bytes accessed | tf_op | source)
XLA Modules:
  0.0 151.3 jit_solution(15256364339088815710)
XLA Ops:
  0.6 0.0 copy-start.3
  0.6 1.4 multiply_reduce_fusion.4
  2.1 0.7 broadcast_in_dim.9
  2.8 15.7 %all-to-all-start.1 = ((bf16[16,16,512]{2,1,0:T(8,128)(2,1)}), bf16[16,16,512]{2,1,0:T(8,128)(2,1)S(1)}, u32[]{:S(2)}, u32[]{:S(2)}) async-start(bf16[16,16,512]{2,1,0:T(8,128)(2,1)} %broadcast_in_dim.9), calls=%async_computation.1 | async-start | bytes 524288 | tf_op jit(solution)/shard_map/all_to_all | solution.py:17
  18.5 0.8 copy.14
  19.3 1.5 %multiply_reduce_fusion.2 = (f32[]{:T(128)}, bf16[8,2048]{1,0:T(8,128)(2,1)S(1)}) fusion(f32[8,2048]{1,0:T(8,128)} %param.8), kind=kLoop, calls=%fused_computation.15 | loop fusion | flops 49151 | bytes 98308 | tf_op jit(solution)/shard_map/reduce_sum | solution.py:74
  20.8 11.5 %all-to-all-done.1 = bf16[16,16,512]{2,1,0:T(8,128)(2,1)S(1)} async-done(((bf16[16,16,512]{2,1,0:T(8,128)(2,1)}), bf16[16,16,512]{2,1,0:T(8,128)(2,1)S(1)}, u32[]{:S(2)}, u32[]{:S(2)}) %all-to-all-start.1) | async-done | bytes 262176 | tf_op jit(solution)/shard_map/all_to_all | solution.py:17
  32.3 1.1 broadcast_in_dim.8
  33.4 12.6 %all-to-all-start = ((bf16[32,8,2048]{2,1,0:T(8,128)(2,1)}), bf16[32,8,2048]{2,1,0:T(8,128)(2,1)S(1)}, u32[]{:S(2)}, u32[]{:S(2)}) async-start(bf16[32,8,2048]{2,1,0:T(8,128)(2,1)} %broadcast_in_dim.8), calls=%async_computation | async-start | bytes 2097152 | tf_op jit(solution)/shard_map/all_to_all | solution.py:17
  46.1 0.0 copy-done.3
  46.1 0.1 copy.13
  46.2 0.1 iota_add_fusion
  46.3 1.4 compare_and_fusion
  47.8 15.4 %all-to-all-done = bf16[32,8,2048]{2,1,0:T(8,128)(2,1)S(1)} async-done(((bf16[32,8,2048]{2,1,0:T(8,128)(2,1)}), bf16[32,8,2048]{2,1,0:T(8,128)(2,1)S(1)}, u32[]{:S(2)}, u32[]{:S(2)}) %all-to-all-start) | async-done | bytes 1048608 | tf_op jit(solution)/shard_map/all_to_all | solution.py:17
  63.1 4.1 %multiply_reduce_fusion = (f32[]{:T(128)}, bf16[2048,512]{1,0:T(8,128)(2,1)S(1)}) fusion(bf16[2048,512]{1,0:T(8,128)(2,1)} %param.5, bf16[256,512]{1,0:T(8,128)(2,1)S(1)} %bitcast.35, bf16[32,8,2048]{2,1,0:T(8,128)(2,1)S(1)} %all-to-all-done, pred[256,8,4,128]{3,2,1,0:T(4,128)(4,1)S(1)} %bitcast.34), kind=kOutput, calls=%fused_computation | convolution fusion | flops 543162368 | bytes 6553604 | tf_op jit(solution)/shard_map/dot_general | solution.py:75
  67.3 0.0 copy-start.4
  67.3 1.5 convolution_convert_fusion.1
  68.7 0.0 copy-done.4
  68.7 5.5 %all-to-all-start.3 = ((bf16[16,16,512]{2,1,0:T(8,128)(2,1)}), bf16[16,16,512]{2,1,0:T(8,128)(2,1)S(1)}, u32[]{:S(2)}, u32[]{:S(2)}) async-start(bf16[16,16,512]{2,1,0:T(8,128)(2,1)} %bitcast.8), calls=%async_computation.3 | async-start | bytes 524288 | tf_op jit(solution)/shard_map/all_to_all | solution.py:41
  74.2 3.4 %fusion = bf16[32,8,2048]{2,1,0:T(8,128)(2,1)} fusion(bf16[256,512]{1,0:T(8,128)(2,1)S(1)} %bitcast.36, bf16[2048,512]{1,0:T(8,128)(2,1)} %copy-done.4), kind=kOutput, calls=%fused_computation.4 | convolution fusion | flops 537395200 | bytes 3407872 | tf_op jit(solution)/shard_map/dot_general | solution.py:83
  77.6 0.0 copy-start.2
  77.6 0.0 copy-start.1
  77.6 0.0 copy-start
  77.6 10.6 %all-to-all-done.3 = bf16[16,16,512]{2,1,0:T(8,128)(2,1)S(1)} async-done(((bf16[16,16,512]{2,1,0:T(8,128)(2,1)}), bf16[16,16,512]{2,1,0:T(8,128)(2,1)S(1)}, u32[]{:S(2)}, u32[]{:S(2)}) %all-to-all-start.3) | async-done | bytes 262176 | tf_op jit(solution)/shard_map/all_to_all | solution.py:41
  88.2 8.8 %all-to-all-start.2 = ((bf16[32,8,2048]{2,1,0:T(8,128)(2,1)}), bf16[32,8,2048]{2,1,0:T(8,128)(2,1)S(1)}, u32[]{:S(2)}, u32[]{:S(2)}) async-start(bf16[32,8,2048]{2,1,0:T(8,128)(2,1)} %fusion), calls=%async_computation.2 | async-start | bytes 2097152 | tf_op jit(solution)/shard_map/all_to_all | solution.py:41
  97.0 0.0 copy-done.2
  97.0 0.6 multiply_reduce_fusion.5
  99.6 0.6 multiply_reduce_fusion.3
  100.3 13.9 %all-to-all-done.2 = bf16[32,8,2048]{2,1,0:T(8,128)(2,1)S(1)} async-done(((bf16[32,8,2048]{2,1,0:T(8,128)(2,1)}), bf16[32,8,2048]{2,1,0:T(8,128)(2,1)S(1)}, u32[]{:S(2)}, u32[]{:S(2)}) %all-to-all-start.2) | async-done | bytes 1048608 | tf_op jit(solution)/shard_map/all_to_all | solution.py:41
  114.1 0.2 convert_reduce_fusion
  114.3 0.6 multiply_reduce_fusion.1
  116.2 0.7 stack.27
  117.0 10.5 %all_to_all.30 = f32[32,1,128]{2,1,0:T(1,128)S(1)} all-to-all(f32[32,1,128]{2,1,0:T(1,128)S(1)} %broadcast_in_dim.10), channel_id=1, replica_groups=mesh['row'=16,'col_0'=4,'col_1'=4,'layer'=2] {'col_0','col_1','layer'}, dimensions={0} | all-to-all | bytes 32768 | tf_op jit(solution)/shard_map/all_to_all | solution.py:17
  127.6 16.9 %all_to_all.31 = f32[16,1,128]{2,1,0:T(1,128)S(1)} all-to-all(f32[16,1,128]{2,1,0:T(1,128)S(1)} %broadcast_in_dim.11), channel_id=1, replica_groups=mesh['row'=16,'col_0'=4,'col_1'=4,'layer'=2] {'row'}, dimensions={0} | all-to-all | bytes 16384 | tf_op jit(solution)/shard_map/all_to_all | solution.py:17
  144.4 0.6 fusion.5
  147.2 0.0 copy-done.1
  147.2 0.6 multiply_subtract_fusion.1
  147.8 0.0 copy-done
  147.8 0.6 multiply_subtract_fusion
  (12 shorter events, 0.1 us)
Async XLA Ops:
  0.6 45.5 %copy-start.3 = (s32[16,4]{0,1:T(4,128)S(1)}, s32[16,4]{0,1:T(4,128)}, u32[]{:S(2)}) copy-start(s32[16,4]{0,1:T(4,128)} %param.6) | copy-start | bytes 772
  2.8 29.5 %all-to-all-start.1 = ((bf16[16,16,512]{2,1,0:T(8,128)(2,1)}), bf16[16,16,512]{2,1,0:T(8,128)(2,1)S(1)}, u32[]{:S(2)}, u32[]{:S(2)}) async-start(bf16[16,16,512]{2,1,0:T(8,128)(2,1)} %broadcast_in_dim.9), calls=%async_computation.1 | async-start | bytes 524288 | tf_op jit(solution)/shard_map/all_to_all | solution.py:17
  33.4 29.7 %all-to-all-start = ((bf16[32,8,2048]{2,1,0:T(8,128)(2,1)}), bf16[32,8,2048]{2,1,0:T(8,128)(2,1)S(1)}, u32[]{:S(2)}, u32[]{:S(2)}) async-start(bf16[32,8,2048]{2,1,0:T(8,128)(2,1)} %broadcast_in_dim.8), calls=%async_computation | async-start | bytes 2097152 | tf_op jit(solution)/shard_map/all_to_all | solution.py:17
  67.3 1.5 copy-start.4
  68.7 19.5 %all-to-all-start.3 = ((bf16[16,16,512]{2,1,0:T(8,128)(2,1)}), bf16[16,16,512]{2,1,0:T(8,128)(2,1)S(1)}, u32[]{:S(2)}, u32[]{:S(2)}) async-start(bf16[16,16,512]{2,1,0:T(8,128)(2,1)} %bitcast.8), calls=%async_computation.3 | async-start | bytes 524288 | tf_op jit(solution)/shard_map/all_to_all | solution.py:41
  77.6 19.4 %copy-start.2 = (s32[16,4]{0,1:T(4,128)S(1)}, s32[16,4]{0,1:T(4,128)}, u32[]{:S(2)}) copy-start(s32[16,4]{0,1:T(4,128)} %param.7) | copy-start | bytes 772
  77.6 69.6 %copy-start.1 = (f32[16,512]{1,0:T(8,128)S(1)}, f32[16,512]{1,0:T(8,128)}, u32[]{:S(2)}) copy-start(f32[16,512]{1,0:T(8,128)} %param.9) | copy-start | bytes 98308
  77.6 70.2 %copy-start = (f32[8,2048]{1,0:T(8,128)S(1)}, f32[8,2048]{1,0:T(8,128)}, u32[]{:S(2)}) copy-start(f32[8,2048]{1,0:T(8,128)} %param.8) | copy-start | bytes 196612
  88.2 25.9 %all-to-all-start.2 = ((bf16[32,8,2048]{2,1,0:T(8,128)(2,1)}), bf16[32,8,2048]{2,1,0:T(8,128)(2,1)S(1)}, u32[]{:S(2)}, u32[]{:S(2)}) async-start(bf16[32,8,2048]{2,1,0:T(8,128)(2,1)} %fusion), calls=%async_computation.2 | async-start | bytes 2097152 | tf_op jit(solution)/shard_map/all_to_all | solution.py:41

commit v2 on v1

--- a/solution.py
+++ b/solution.py
@@ -69,7 +69,7 @@
     user_low = user_factor.astype(jnp.bfloat16)
     item_low = item_factor.astype(jnp.bfloat16)
     item_cols = gather_directly(item_low, "row", 0)
-    user_rows = gather_directly(user_low, COL_LAYER, 0)
+    user_rows = lax.all_gather(user_low, COL_LAYER, axis=0, tiled=True)
     count_local = jnp.sum(tile_mask * tile_counts).astype(jnp.float32)
     factor_local = jnp.sum(user_factor * user_factor) + jnp.sum(item_factor * item_factor)
     predicted = lax.dot_general(
@@ -83,9 +83,10 @@
     user_share = lax.dot_general(
         item_cols, scaled, (((1,), (1,)), ((), ())), preferred_element_type=jnp.float32
     )
-    user_arrived = sent(user_share.astype(jnp.bfloat16), COL_LAYER, 0)
+    raw_user = lax.psum_scatter(
+        user_share.astype(jnp.bfloat16), COL_LAYER, scatter_dimension=0, tiled=True
+    ).astype(jnp.float32)
     raw_item = summed(item_arrived)
-    raw_user = summed(user_arrived)
     gradient_local = jnp.sum(raw_user * raw_user) + jnp.sum(raw_item * raw_item)
     count_sum, factor_sum, error_sum, gradient_sum = scalars_summed(
         [count_local, factor_local, error_local, gradient_local]

time: 152 us -> 237 us (1.56)
  waiting for transfers between devices: 51.4 us -> 136 us
  between operations: 9.06 us -> 22.5 us
  blocking collectives: 27.4 us -> 14.3 us
  local copies, waits for them, and re-layouts: 4.06 us -> 7.32 us
  starting transfers between devices: 42.6 us -> 40 us
    unnamed x0 -> x3, waiting for transfers between devices: none -> 68.7 us
    all_gather x0 -> x1, waiting for transfers between devices: none -> 34.2 us  [body(): user_rows = lax.all_gather(user_low, COL_LAYER, axis=0, tiled=True)]
    all_to_all x2 -> x1, blocking collectives: 27.4 us -> 14.3 us  [from_everyone(): lax.all_to_all(jnp.broadcast_to(array[None], (count, *array.shape)), axis...]
    all_to_all x2 -> x1, waiting for transfers between devices: 24.5 us -> 11.5 us  [sent(): return lax.all_to_all(blocks, axis, split_axis=0, concat_axis=0, tiled=True)]
    all_to_all x2, waiting for transfers between devices: 26.9 us -> 21.5 us  [from_everyone(): lax.all_to_all(jnp.broadcast_to(array[None], (count, *array.shape)), axis...]
    unnamed x11 -> x13, local copies, waits for them, and re-layouts: 0.78 us -> 4.52 us
    dot_general x1, matrix products: 3.35 us -> 0.73 us  [body(): lax.dot_general(item_cols, scaled, (((1,), (1,)), ((), ())), preferred_el...]
    all_to_all x2 -> x1, starting transfers between devices: 14.3 us -> 12.2 us  [sent(): return lax.all_to_all(blocks, axis, split_axis=0, concat_axis=0, tiled=True)]
  transfers between devices with their start and end apart: 4 -> 5, of which waited for: 4 -> 5; matrix products, arithmetic and copies ran while one was open for 6% -> 4% of each run, Pallas kernels for 0% -> 0%
where the time goes in v2:
time: 237 us
  waiting for transfers between devices  136 us (57%)
  starting transfers between devices  40 us (17%)
  between operations  22.5 us (9%)
  blocking collectives  14.3 us (6%)
  other arithmetic  8.72 us (4%)
  matrix products  7.83 us (3%)
  local copies, waits for them, and re-layouts  7.32 us (3%)
    unnamed x3, waiting for transfers between devices  68.7 us
    all_gather x1, waiting for transfers between devices, body(): user_rows = lax.all_gather(user_low, COL_LAYER, axis=0, tiled=True)  34.2 us
    all_to_all x2, starting transfers between devices, from_everyone(): lax.all_to_all(jnp.broadcast_to(array[None], (count, *array.shape)), axis...  27.7 us
    all_to_all x2, waiting for transfers between devices, from_everyone(): lax.all_to_all(jnp.broadcast_to(array[None], (count, *array.shape)), axis...  21.5 us
    all_to_all x1, blocking collectives, from_everyone(): lax.all_to_all(jnp.broadcast_to(array[None], (count, *array.shape)), axis...  14.3 us
    all_to_all x1, starting transfers between devices, sent(): return lax.all_to_all(blocks, axis, split_axis=0, concat_axis=0, tiled=True)  12.2 us
    all_to_all x1, waiting for transfers between devices, sent(): return lax.all_to_all(blocks, axis, split_axis=0, concat_axis=0, tiled=True)  11.5 us
  transfers between devices with their start and end apart: 5, of which 5 were waited for; matrix products, arithmetic and copies ran while one was open for 4% of the time, Pallas kernels for 0%

profile of v2, /device:TPU:1, one launch (start us, length us, event | category | flops | bytes accessed | tf_op | source)
XLA Modules:
  0.0 236.5 jit_solution(11960499413413975167)
XLA Ops:
  7.2 0.0 all-gather.2.cloned.1.call-start
  7.2 2.1 multiply_reduce_fusion.1
  9.3 0.0 all-gather.2.cloned.1.call-update
  9.4 1.4 multiply_reduce_fusion.3
  10.8 0.7 broadcast_in_dim.6
  11.6 15.7 %all-to-all-start = ((bf16[16,16,512]{2,1,0:T(8,128)(2,1)}), bf16[16,16,512]{2,1,0:T(8,128)(2,1)S(1)}, u32[]{:S(2)}, u32[]{:S(2)}) async-start(bf16[16,16,512]{2,1,0:T(8,128)(2,1)} %broadcast_in_dim.6), calls=%async_computation | async-start | bytes 524288 | tf_op jit(solution)/shard_map/all_to_all | solution.py:17
  27.3 0.0 reduce-scatter.4.cloned.1.call-start
  27.4 0.8 copy.22
  28.1 0.7 broadcast_compare_fusion
  28.8 0.1 copy.21
  28.9 0.1 iota_add_fusion
  29.0 1.4 compare_and_fusion
  30.4 10.6 %all-to-all-done = bf16[16,16,512]{2,1,0:T(8,128)(2,1)S(1)} async-done(((bf16[16,16,512]{2,1,0:T(8,128)(2,1)}), bf16[16,16,512]{2,1,0:T(8,128)(2,1)S(1)}, u32[]{:S(2)}, u32[]{:S(2)}) %all-to-all-start) | async-done | bytes 262176 | tf_op jit(solution)/shard_map/all_to_all | solution.py:17
  41.1 34.2 %all-gather.2.cloned.1.call-done = bf16[256,2048]{1,0:T(8,128)(2,1)} async-done(((bf16[8,2048]{1,0:T(8,128)(2,1)}), bf16[256,2048]{1,0:T(8,128)(2,1)}) %all-gather.2.cloned.1.call-update) | async-done | bytes 1048592 | tf_op jit(solution)/shard_map/all_gather | solution.py:72
  75.2 4.4 %multiply_reduce_fusion = (f32[]{:T(128)}, bf16[2048,512]{1,0:T(8,128)(2,1)S(1)}) fusion(bf16[2048,512]{1,0:T(8,128)(2,1)} %param.5, bf16[256,2048]{1,0:T(8,128)(2,1)} %all-gather.2.cloned.1.call-done, bf16[256,512]{1,0:T(8,128)(2,1)S(1)} %bitcast.29, pred[256,8,4,128]{3,2,1,0:T(4,128)(4,1)S(1)} %bitcast.28), kind=kOutput, calls=%fused_computation | convolution fusion | flops 543162368 | bytes 6553604 | tf_op jit(solution)/shard_map/dot_general | solution.py:75
  79.7 0.7 fusion
  80.4 1.4 copy.27
  81.8 0.0 reduce-scatter.4.cloned.1.call-update
  81.9 0.0 copy-start.2
  81.9 0.0 copy-start.3
  81.9 0.0 copy-start
  81.9 2.7 %convolution_convert_fusion.1 = bf16[512,256]{0,1:T(8,128)(2,1)} fusion(bf16[256,2048]{1,0:T(8,128)(2,1)} %all-gather.2.cloned.1.call-done, bf16[2048,512]{1,0:T(8,128)(2,1)S(1)} %get-tuple-element.29), kind=kOutput, calls=%fused_computation.7 | convolution fusion | flops 537001984 | bytes 3407872 | tf_op jit(solution)/shard_map/dot_general | solution.py:81
  84.6 0.0 copy-start.1
  84.6 12.2 %all-to-all-start.1 = ((bf16[16,16,512]{2,1,0:T(8,128)(2,1)}), bf16[16,16,512]{2,1,0:T(8,128)(2,1)S(1)}, u32[]{:S(2)}, u32[]{:S(2)}) async-start(bf16[16,16,512]{2,1,0:T(8,128)(2,1)} %bitcast.6), calls=%async_computation.1 | async-start | bytes 524288 | tf_op jit(solution)/shard_map/all_to_all | solution.py:41
  96.7 0.0 copy-done.2
  96.8 0.0 copy-done.3
  96.8 0.6 multiply_reduce_fusion.4
  99.3 11.5 %all-to-all-done.1 = bf16[16,16,512]{2,1,0:T(8,128)(2,1)S(1)} async-done(((bf16[16,16,512]{2,1,0:T(8,128)(2,1)}), bf16[16,16,512]{2,1,0:T(8,128)(2,1)S(1)}, u32[]{:S(2)}, u32[]{:S(2)}) %all-to-all-start.1) | async-done | bytes 262176 | tf_op jit(solution)/shard_map/all_to_all | solution.py:41
  110.9 0.6 multiply_reduce_fusion.2
  111.5 68.7 %reduce-scatter.4.cloned.1.call-done = bf16[8,2048]{1,0:T(8,128)(2,1)} async-done(((bf16[256,2048]{1,0:T(8,128)(2,1)}), bf16[8,2048]{1,0:T(8,128)(2,1)}) %reduce-scatter.4.cloned.1.call-update) | async-done | bytes 32784
  180.2 1.0 copy.28
  181.2 0.9 fusion.1
  183.4 0.7 stack.27
  184.2 14.3 %all_to_all.20 = f32[32,1,128]{2,1,0:T(1,128)S(1)} all-to-all(f32[32,1,128]{2,1,0:T(1,128)S(1)} %broadcast_in_dim.7), channel_id=1, replica_groups=mesh['row'=16,'col_0'=4,'col_1'=4,'layer'=2] {'col_0','col_1','layer'}, dimensions={0} | all-to-all | bytes 32768 | tf_op jit(solution)/shard_map/all_to_all | solution.py:17
  198.5 0.6 broadcast_in_dim.8
  199.1 12.0 %all-to-all-start.3 = ((f32[16,1,128]{2,1,0:T(1,128)}), f32[16,1,128]{2,1,0:T(1,128)S(1)}, u32[]{:S(2)}, u32[]{:S(2)}) async-start(f32[16,1,128]{2,1,0:T(1,128)} %broadcast_in_dim.8), calls=%async_computation.3 | async-start | bytes 16384 | tf_op jit(solution)/shard_map/all_to_all | solution.py:17
  211.1 0.0 copy-done
  211.1 0.3 copy.25
  211.4 10.9 %all-to-all-done.3 = f32[16,1,128]{2,1,0:T(1,128)S(1)} async-done(((f32[16,1,128]{2,1,0:T(1,128)}), f32[16,1,128]{2,1,0:T(1,128)S(1)}, u32[]{:S(2)}, u32[]{:S(2)}) %all-to-all-start.3) | async-done | bytes 8224 | tf_op jit(solution)/shard_map/all_to_all | solution.py:17
  222.4 0.6 fusion.5
  225.1 0.0 copy-done.1
  225.1 0.6 multiply_subtract_fusion
  225.7 0.1 fusion.2
  225.8 0.9 copy.26
  (10 shorter events, 0.1 us)
Async XLA Ops:
  7.2 68.1 %all-gather.2.cloned.1.call-start = ((), (), s32[]{:S(2)}) async-start(), calls=%async_computation.5 | async-start | bytes 1081344 | tf_op jit(solution)/shard_map/all_gather | solution.py:72
  11.6 29.5 %all-to-all-start = ((bf16[16,16,512]{2,1,0:T(8,128)(2,1)}), bf16[16,16,512]{2,1,0:T(8,128)(2,1)S(1)}, u32[]{:S(2)}, u32[]{:S(2)}) async-start(bf16[16,16,512]{2,1,0:T(8,128)(2,1)} %broadcast_in_dim.6), calls=%async_computation | async-start | bytes 524288 | tf_op jit(solution)/shard_map/all_to_all | solution.py:17
  27.3 152.9 %reduce-scatter.4.cloned.1.call-start = ((), (), s32[]{:S(2)}) async-start(), calls=%async_computation.6 | async-start | bytes 1081344
  81.9 14.9 %copy-start.2 = (s32[16,4]{0,1:T(4,128)S(1)}, s32[16,4]{0,1:T(4,128)}, u32[]{:S(2)}) copy-start(s32[16,4]{0,1:T(4,128)} %param.7) | copy-start | bytes 772
  81.9 14.9 %copy-start.3 = (s32[16,4]{0,1:T(4,128)S(1)}, s32[16,4]{0,1:T(4,128)}, u32[]{:S(2)}) copy-start(s32[16,4]{0,1:T(4,128)} %param.6) | copy-start | bytes 772
  81.9 129.2 %copy-start = (f32[8,2048]{1,0:T(8,128)S(1)}, f32[8,2048]{1,0:T(8,128)}, u32[]{:S(2)}) copy-start(f32[8,2048]{1,0:T(8,128)} %param.8) | copy-start | bytes 196612
  84.6 140.5 %copy-start.1 = (f32[16,512]{1,0:T(8,128)S(1)}, f32[16,512]{1,0:T(8,128)}, u32[]{:S(2)}) copy-start(f32[16,512]{1,0:T(8,128)} %param.9) | copy-start | bytes 98308
  84.6 26.3 %all-to-all-start.1 = ((bf16[16,16,512]{2,1,0:T(8,128)(2,1)}), bf16[16,16,512]{2,1,0:T(8,128)(2,1)S(1)}, u32[]{:S(2)}, u32[]{:S(2)}) async-start(bf16[16,16,512]{2,1,0:T(8,128)(2,1)} %bitcast.6), calls=%async_computation.1 | async-start | bytes 524288 | tf_op jit(solution)/shard_map/all_to_all | solution.py:41
  199.1 23.3 %all-to-all-start.3 = ((f32[16,1,128]{2,1,0:T(1,128)}), f32[16,1,128]{2,1,0:T(1,128)S(1)}, u32[]{:S(2)}, u32[]{:S(2)}) async-start(f32[16,1,128]{2,1,0:T(1,128)} %broadcast_in_dim.8), calls=%async_computation.3 | async-start | bytes 16384 | tf_op jit(solution)/shard_map/all_to_all | solution.py:17
Sparse Core Ops, SparseCore 0:
  11.7 63.5 all-gather.1
  82.0 98.1 reduce-scatter.3

commit v3 on v1

v3 whole, which is shorter than its diff:
```python
import jax
import jax.numpy as jnp
from jax import lax
from jax.experimental import pallas as pl
from jax.experimental.pallas import tpu as pltpu
from jax.sharding import Mesh
from jax.sharding import PartitionSpec as P

TILE = 128
LANES = 128
STRIPE = 256
COL_LAYER = ("col_0", "col_1", "layer")
VMEM = pl.BlockSpec(memory_space=pltpu.VMEM)
SMEM = pl.BlockSpec(memory_space=pltpu.SMEM)
ANYWHERE = pl.BlockSpec(memory_space=pl.ANY)
GRANT = pltpu.CompilerParams(vmem_limit_bytes=16 * 2**20)

epsilon = 1e-12
trust_ratio = 0.2


def turned_by_core(pair, layer):
    half = pair.shape[-2] // 2
    swapped = jnp.concatenate([pair[half:], pair[:half]], axis=0)
    return jnp.where(layer == 1, swapped, pair)


def lower_body(layer_ref, user_ref, item_ref, user_low_ref, item_blocks_ref):
    user_low_ref[...] = user_ref[...].astype(jnp.bfloat16)
    item = turned_by_core(item_ref[...], layer_ref[0]).astype(jnp.bfloat16)
    item_blocks_ref[...] = jnp.broadcast_to(item[None], item_blocks_ref.shape)


def lowered(layer, user_factor, item_factor, rows):
    return pl.pallas_call(
        lower_body,
        in_specs=[SMEM, VMEM, VMEM],
        out_specs=[VMEM, VMEM],
        out_shape=[
            jax.ShapeDtypeStruct(user_factor.shape, jnp.bfloat16),
            jax.ShapeDtypeStruct((rows, *item_factor.shape), jnp.bfloat16),
        ],
        compiler_params=GRANT,
        name="lower",
    )(layer, user_factor, item_factor)


def own_halves_first(blocks):
    count, pair, columns = blocks.shape
    halves = [blocks[:, : pair // 2], blocks[:, pair // 2 :]]
    return jnp.concatenate([half.reshape(count * pair // 2, columns) for half in halves], axis=0)


def residual_body(
    mask_ref, counts_ref, mine_ref, other_ref, item_blocks_ref, far_ratings_ref,
    scaled_ref, item_share_ref, item_ref, error_ref, user_ref, ratings_ref, total_ref, user_sems, ratings_sems,
):
    rank_half = mine_ref.shape[0]
    user_copies = [
        pltpu.make_async_copy(half_ref, user_ref.at[pl.ds(at * rank_half, rank_half)], user_sems.at[at])
        for at, half_ref in enumerate((mine_ref, other_ref))
    ]
    stripes = range(0, ratings_ref.shape[0], STRIPE)
    ratings_copies = [
        pltpu.make_async_copy(
            far_ratings_ref.at[pl.ds(start, STRIPE)], ratings_ref.at[pl.ds(start, STRIPE)], ratings_sems.at[at]
        )
        for at, start in enumerate(stripes)
    ]
    for copy in user_copies + ratings_copies:
        copy.start()
    item_ref[...] = own_halves_first(item_blocks_ref[...])
    item = item_ref[...]
    for copy in user_copies:
        copy.wait()
    side = (TILE, TILE)
    position = lax.broadcasted_iota(jnp.int32, side, 0) * TILE + lax.broadcasted_iota(jnp.int32, side, 1)
    columns = ratings_ref.shape[1]
    for start, copy in zip(stripes, ratings_copies):
        stripe = pl.ds(start, STRIPE)
        user = user_ref[:, stripe]
        predicted = lax.dot_general(user, item, (((0,), (0,)), ((), ())), preferred_element_type=jnp.float32)
        copy.wait()
        for row in range(0, STRIPE, TILE):
            for column in range(0, columns, TILE):
                tile_at = (column // TILE, (start + row) // TILE)
                limit = jnp.where(mask_ref[tile_at] == 1, counts_ref[tile_at], 0)
                rows, cols = pl.ds(start + row, TILE), pl.ds(column, TILE)
                difference = predicted[row : row + TILE, column : column + TILE] - ratings_ref[rows, cols].astype(
                    jnp.float32
                )
                residual = jnp.where(position < limit, difference, 0.0)
                scaled_ref[rows, cols] = residual.astype(jnp.bfloat16)
                error = (residual * residual).reshape(TILE // 8, 8, TILE).sum(axis=0)
                if start + row == 0:
                    error_ref[:, cols] = error
                else:
                    error_ref[:, cols] += error
        share = jnp.dot(user, scaled_ref[stripe], preferred_element_type=jnp.float32)
        if start == 0:
            total_ref[...] = share
        else:
            total_ref[...] += share
    count, pair, _ = item_share_ref.shape
    half = pair // 2
    share = total_ref[...].astype(jnp.bfloat16)
    for part in range(2):
        rows = share[part * rank_half : (part + 1) * rank_half]
        item_share_ref[:, part * half : (part + 1) * half] = rows.reshape(count, half, columns)


def residual_of(mask, counts, mine, other, item_blocks, ratings):
    rank, columns = 2 * mine.shape[0], ratings.shape[1]
    flops = 4 * rank * ratings.shape[0] * columns
    return pl.pallas_call(
        residual_body,
        in_specs=[SMEM, SMEM, ANYWHERE, ANYWHERE, VMEM, ANYWHERE],
        out_specs=[VMEM] * 4,
        out_shape=[
            jax.ShapeDtypeStruct(ratings.shape, jnp.bfloat16),
            jax.ShapeDtypeStruct(item_blocks.shape, jnp.bfloat16),
            jax.ShapeDtypeStruct((rank, columns), jnp.bfloat16),
            jax.ShapeDtypeStruct((8, columns), jnp.float32),
        ],
        scratch_shapes=[
            pltpu.VMEM((rank, ratings.shape[0]), jnp.bfloat16),
            pltpu.VMEM(ratings.shape, jnp.bfloat16),
            pltpu.VMEM((rank, columns), jnp.float32),
            pltpu.SemaphoreType.DMA((2,)),
            pltpu.SemaphoreType.DMA((ratings.shape[0] // STRIPE,)),
        ],
        cost_estimate=pl.CostEstimate(flops=flops, bytes_accessed=4 * ratings.size, transcendentals=0),
        compiler_params=GRANT,
        name="residual",
    )(mask, counts, mine, other, item_blocks, ratings)


def user_share_body(item_ref, scaled_ref, mine_ref, other_ref):
    half = mine_ref.shape[0]
    item = item_ref[...]
    for start in range(0, scaled_ref.shape[0], STRIPE):
        stripe = pl.ds(start, STRIPE)
        share = lax.dot_general(
            item, scaled_ref[stripe], (((1,), (1,)), ((), ())), preferred_element_type=jnp.float32
        ).astype(jnp.bfloat16)
        mine_ref[:, stripe] = share[:half]
        other_ref[:, stripe] = share[half:]


def user_share_of(item, scaled):
    shape = jax.ShapeDtypeStruct((item.shape[0] // 2, scaled.shape[0]), jnp.bfloat16)
    return pl.pallas_call(
        user_share_body,
        in_specs=[VMEM, VMEM],
        out_specs=[VMEM, VMEM],
        out_shape=[shape, shape],
        cost_estimate=pl.CostEstimate(flops=2 * item.shape[0] * scaled.size, bytes_accessed=0, transcendentals=0),
        compiler_params=GRANT,
        name="user_share",
    )(item, scaled)


def halves_body(col_ref, mine_ref, arrived_ref, *block_refs):
    count = mine_ref.shape[0]
    for by, block_ref in enumerate(block_refs):
        at = lax.rem(col_ref[0] + by, count)
        block = mine_ref[at].astype(jnp.float32) + arrived_ref[at].astype(jnp.float32)
        block_ref[...] = block.astype(jnp.bfloat16)


def halves_summed(col, mine, arrived):
    count, *block = mine.shape
    shape = jax.ShapeDtypeStruct(tuple(block), jnp.bfloat16)
    return pl.pallas_call(
        halves_body,
        in_specs=[SMEM, VMEM, VMEM],
        out_specs=[VMEM] * count,
        out_shape=[shape] * count,
        compiler_params=GRANT,
        name="halves",
    )(col, mine, arrived)


def blocks_body(*refs):
    *block_refs, total_ref = refs
    total = block_refs[0][...].astype(jnp.float32)
    for block_ref in block_refs[1:]:
        total = total + block_ref[...].astype(jnp.float32)
    total_ref[...] = total.astype(jnp.bfloat16)


def blocks_summed(blocks):
    return pl.pallas_call(
        blocks_body,
        in_specs=[VMEM] * len(blocks),
        out_specs=VMEM,
        out_shape=jax.ShapeDtypeStruct(blocks[0].shape, jnp.bfloat16),
        compiler_params=GRANT,
        name="blocks",
    )(*blocks)


def summed(blocks_ref):
    total = blocks_ref[0].astype(jnp.float32)
    for i in range(1, blocks_ref.shape[0]):
        total = total + blocks_ref[i].astype(jnp.float32)
    return total


def item_raw_body(layer_ref, mask_ref, counts_ref, arrived_ref, user_ref, item_ref, error_ref, raw_ref, sums_ref):
    raw = summed(arrived_ref)
    raw_ref[...] = turned_by_core(raw, layer_ref[0])
    user, item = user_ref[...], item_ref[...]
    lane = lax.broadcasted_iota(jnp.int32, sums_ref.shape, 1)
    sums = jnp.zeros(sums_ref.shape, jnp.float32)
    for at, value in enumerate(
        (
            jnp.sum((mask_ref[...] * counts_ref[...]).astype(jnp.float32)),
            jnp.sum(user * user) + jnp.sum(item * item),
            jnp.sum(error_ref[...]),
            jnp.sum(raw * raw),
        )
    ):
        sums = jnp.where(lane == at, value, sums)
    sums_ref[...] = sums


def item_raw_of(layer, mask, counts, arrived, user_factor, item_factor, error):
    return pl.pallas_call(
        item_raw_body,
        in_specs=[SMEM] + [VMEM] * 6,
        out_specs=[VMEM, VMEM],
        out_shape=[
            jax.ShapeDtypeStruct(arrived.shape[1:], jnp.float32),
            jax.ShapeDtypeStruct((1, LANES), jnp.float32),
        ],
        compiler_params=GRANT,
        name="item_raw",
    )(layer, mask, counts, arrived, user_factor, item_factor, error)


def user_raw_body(arrived_ref, sums_ref, raw_ref, packed_ref):
    raw = summed(arrived_ref)
    raw_ref[...] = raw
    lane = lax.broadcasted_iota(jnp.int32, sums_ref.shape, 1)
    sums = sums_ref[...] + jnp.where(lane == 3, jnp.sum(raw * raw), 0.0)
    packed_ref[...] = jnp.broadcast_to(sums[None], packed_ref.shape)


def user_raw_of(arrived, sums, devices):
    return pl.pallas_call(
        user_raw_body,
        in_specs=[VMEM, VMEM],
        out_specs=[VMEM, VMEM],
        out_shape=[
            jax.ShapeDtypeStruct(arrived.shape[1:], jnp.float32),
            jax.ShapeDtypeStruct((devices, *sums.shape), jnp.float32),
        ],
        compiler_params=GRANT,
        name="user_raw",
    )(arrived, sums)


def packed_again_body(arrived_ref, packed_ref):
    packed_ref[...] = jnp.broadcast_to(summed(arrived_ref)[None], packed_ref.shape)


def packed_again(arrived, devices):
    return pl.pallas_call(
        packed_again_body,
        in_specs=[VMEM],
        out_specs=VMEM,
        out_shape=jax.ShapeDtypeStruct((devices, *arrived.shape[1:]), jnp.float32),
        compiler_params=GRANT,
        name="packed_again",
    )(arrived)


def step_body(arrived_ref, user_ref, item_ref, raw_user_ref, raw_item_ref, new_user_ref, new_item_ref, ends_ref):
    sums = summed(arrived_ref)
    lane = lax.broadcasted_iota(jnp.int32, sums.shape, 1)

    def lane_at(at):
        return jnp.sum(jnp.where(lane == at, sums, 0.0), axis=1, keepdims=True)

    observed_total = jnp.maximum(lane_at(0), 1.0)
    scale = 2.0 / observed_total
    grad_norm = scale * jnp.sqrt(lane_at(3) + epsilon)
    step_size = trust_ratio * jnp.sqrt(lane_at(1) + epsilon) / grad_norm * scale
    new_user_ref[...] = user_ref[...] - step_size * raw_user_ref[...]
    new_item_ref[...] = item_ref[...] - step_size * raw_item_ref[...]
    ends_ref[...] = jnp.where(lane == 0, lane_at(2) / observed_total, grad_norm)


def stepped(arrived, user_factor, item_factor, raw_user, raw_item):
    return pl.pallas_call(
        step_body,
        in_specs=[VMEM] * 5,
        out_specs=[VMEM] * 3,
        out_shape=[
            jax.ShapeDtypeStruct(user_factor.shape, jnp.float32),
            jax.ShapeDtypeStruct(item_factor.shape, jnp.float32),
            jax.ShapeDtypeStruct(arrived.shape[1:], jnp.float32),
        ],
        compiler_params=GRANT,
        name="step",
    )(arrived, user_factor, item_factor, raw_user, raw_item)


def exchanged(blocks, axis):
    return lax.all_to_all(blocks, axis, 0, 0, tiled=True)


def shifted(array, axis, by):
    count = lax.axis_size(axis)
    return lax.ppermute(array, axis, [(i, (i + by) % count) for i in range(count)])


def body(ratings, tile_mask, tile_counts, user_factor, item_factor):
    rows, width = lax.axis_size("row"), lax.axis_size("col_0")
    layer, col_0 = (lax.axis_index(axis).astype(jnp.int32)[None] for axis in ("layer", "col_0"))
    mask, counts = tile_mask.T, tile_counts.T
    user_low, item_blocks = lowered(layer, user_factor, item_factor, rows)
    item_blocks = exchanged(item_blocks, "row")
    mine = lax.all_gather(user_low, ("col_0", "col_1"), axis=0, tiled=True)
    other = shifted(mine, "layer", 1)
    scaled, item_share, item, error = residual_of(mask, counts, mine, other, item_blocks, ratings)
    item_arrived = exchanged(item_share, "row")
    my_share, other_share = user_share_of(item, scaled)
    partner_share = shifted(other_share, "layer", 1)
    blocked = (width, user_factor.shape[0] * width, user_factor.shape[1])
    blocks = halves_summed(col_0, my_share.reshape(blocked), partner_share.reshape(blocked))
    blocks = [blocks[0]] + [shifted(blocks[by], "col_0", by) for by in range(1, width)]
    quarter = blocks_summed(blocks)
    user_arrived = exchanged(quarter.reshape(width, *user_factor.shape), "col_1")
    raw_item, sums = item_raw_of(layer, mask, counts, item_arrived, user_factor, item_factor, error)
    raw_user, packed = user_raw_of(user_arrived, sums, lax.axis_size(COL_LAYER))
    packed = exchanged(packed, COL_LAYER)
    packed = packed_again(packed, rows)
    packed = exchanged(packed, "row")
    new_user, new_item, ends = stepped(packed, user_factor, item_factor, raw_user, raw_item)
    return (new_user, new_item, ends[0, 0], ends[0, 1])


def solution(mesh):
    finer = Mesh(
        mesh.devices.reshape(mesh.shape["row"], 4, 4, mesh.shape["layer"]),
        ("row", "col_0", "col_1", "layer"),
    )
    return jax.shard_map(
        body,
        mesh=finer,
        in_specs=(
            P("row", COL_LAYER),
            P("row", COL_LAYER),
            P("row", COL_LAYER),
            P(COL_LAYER, "row"),
            P("row", COL_LAYER),
        ),
        out_specs=(P(COL_LAYER, "row"), P("row", COL_LAYER), P(), P()),
        check_vma=False,
    )
```

time: 152 us -> 137 us (0.901)
  waiting for transfers between devices: 51.4 us -> 10.8 us
  blocking collectives: 27.4 us -> 56.9 us
  Pallas kernels: 0 us -> 9.62 us
  matrix products: 8.94 us -> 0 us
  starting transfers between devices: 42.6 us -> 51 us
  between operations: 9.06 us -> 0.79 us
  other arithmetic: 7.87 us -> 0 us
  local copies, waits for them, and re-layouts: 4.06 us -> 7 us
    all_to_all x4 -> x3, waiting for transfers between devices: 51.4 us -> 4.63 us  [exchanged(): return lax.all_to_all(blocks, axis, 0, 0, tiled=True)]
    ppermute x0 -> x5, starting transfers between devices: none -> 20 us  [shifted(): lax.ppermute(array, axis, [(i, (i + by) % count) for i in range(count)])]
    all_gather x0 -> x1, blocking collectives: none -> 19.9 us  [body(): mine = lax.all_gather(user_low, ('col_0', 'col_1'), axis=0, tiled=True)]
    all_to_all x4 -> x3, starting transfers between devices: 42.6 us -> 31 us  [exchanged(): return lax.all_to_all(blocks, axis, 0, 0, tiled=True)]
    pallas_call x0 -> x9, Pallas kernels: none -> 9.62 us  [the longest x1 5.36 us: residual_of(): pl.pallas_call(residual_body, in_specs=[SMEM, SMEM, ANYWHERE, ANYWHERE, V...]
    all_to_all x2, blocking collectives: 27.4 us -> 37 us  [exchanged(): return lax.all_to_all(blocks, axis, 0, 0, tiled=True)]
    dot_general x3 -> x0, matrix products: 8.94 us -> none  [the longest x1 4.13 us: body(): lax.dot_general(user_rows, item_cols, (((0,), (0,)), ((), ())), preferred...]
    ppermute x0 -> x5, waiting for transfers between devices: none -> 6.19 us  [shifted(): lax.ppermute(array, axis, [(i, (i + by) % count) for i in range(count)])]
  transfers between devices with their start and end apart: 4 -> 8, of which waited for: 4 -> 5; matrix products, arithmetic and copies ran while one was open for 6% -> 0% of each run, Pallas kernels for 0% -> 2%
where the time goes in v3:
time: 137 us; the launch traced here: 136 us
  blocking collectives  56.9 us (42%)
  starting transfers between devices  51 us (37%)
  waiting for transfers between devices  10.8 us (8%)
  Pallas kernels  9.62 us (7%)
  local copies, waits for them, and re-layouts  7 us (5%)
    all_to_all x2, blocking collectives, exchanged(): return lax.all_to_all(blocks, axis, 0, 0, tiled=True)  37 us
    all_to_all x3, starting transfers between devices, exchanged(): return lax.all_to_all(blocks, axis, 0, 0, tiled=True)  31 us
    ppermute x5, starting transfers between devices, shifted(): lax.ppermute(array, axis, [(i, (i + by) % count) for i in range(count)])  20 us
    all_gather x1, blocking collectives, body(): mine = lax.all_gather(user_low, ('col_0', 'col_1'), axis=0, tiled=True)  19.9 us
    unnamed x22, local copies, waits for them, and re-layouts  6.42 us
    ppermute x5, waiting for transfers between devices, shifted(): lax.ppermute(array, axis, [(i, (i + by) % count) for i in range(count)])  6.19 us
    pallas_call x1, Pallas kernels, residual_of(): pl.pallas_call(residual_body, in_specs=[SMEM, SMEM, ANYWHERE, ANYWHERE, V...  5.36 us
    all_to_all x3, waiting for transfers between devices, exchanged(): return lax.all_to_all(blocks, axis, 0, 0, tiled=True)  4.63 us
  transfers between devices with their start and end apart: 8, of which 5 were waited for; matrix products, arithmetic and copies ran while one was open for 0% of the time, Pallas kernels for 2%

profile of v3, /device:TPU:1, one launch (start us, length us, event | category | flops | bytes accessed | tf_op | source)
XLA Modules:
  0.0 136.2 jit_solution(11405258793985186029)
XLA Ops:
  0.6 0.0 copy-start
  0.6 0.8 copy-done
  1.5 0.0 copy-start.2
  1.5 0.8 copy-done.2
  2.2 0.7 lower.1
  3.0 15.7 %all-to-all-start = ((bf16[16,16,512]{2,1,0:T(8,128)(2,1)}), bf16[16,16,512]{2,1,0:T(8,128)(2,1)S(1)}, u32[]{:S(2)}, u32[]{:S(2)}) async-start(bf16[16,16,512]{2,1,0:T(8,128)(2,1)} %get-tuple-element.24), calls=%async_computation | async-start | bytes 524288 | tf_op jit(solution)/shard_map/all_to_all | solution.py:311
  18.7 19.9 %all_gather.3.mine_ref = bf16[128,2048]{1,0:T(8,128)(2,1)S(1)} all-gather(bf16[8,2048]{1,0:T(8,128)(2,1)S(1)} %get-tuple-element.23), channel_id=1, replica_groups=mesh['row'=16,'col_0'=4,'col_1'=4,'layer'=2] {'col_0','col_1'}, dimensions={0}, use_global_device_ids=true | all-gather | bytes 557056 | tf_op jit(solution)/shard_map/all_gather | solution.py:325
  38.7 7.3 %collective-permute-start = (bf16[128,2048]{1,0:T(8,128)(2,1)S(1)}, bf16[128,2048]{1,0:T(8,128)(2,1)S(1)}, u32[]{:S(2)}, u32[]{:S(2)}) collective-permute-start(bf16[128,2048]{1,0:T(8,128)(2,1)S(1)} %all_gather.3.mine_ref), channel_id=1, source_target_pairs={{0,1},{1,0},{2,3},{3,2},{4,5},{5,4},{6,7},{7,6},{8,9},{9,8},{10,11... | collective-permute-start | bytes 1572872 | tf_op jit(solution)/shard_map/ppermute | solution.py:316
  46.0 1.5 %collective-permute-done.other_ref = bf16[128,2048]{1,0:T(8,128)(2,1)S(1)} collective-permute-done((bf16[128,2048]{1,0:T(8,128)(2,1)S(1)}, bf16[128,2048]{1,0:T(8,128)(2,1)S(1)}, u32[]{:S(2)}, u32[]{:S(2)}) %collective-permute-start) | collective-permute-done | bytes 524320 | tf_op jit(solution)/shard_map/ppermute | solution.py:316
  47.5 0.0 copy-start.9
  47.5 0.8 copy-done.9
  48.3 0.0 all-to-all-done.item_blocks_ref
  48.3 0.0 copy-start.4
  48.3 0.7 copy-done.4
  49.0 0.0 copy-start.6
  49.0 0.7 copy-done.6
  49.7 0.0 copy-start.8
  49.7 1.6 %copy-done.8 = bf16[2048,512]{1,0:T(8,128)(2,1)S(1)} copy-done((bf16[2048,512]{1,0:T(8,128)(2,1)S(1)}, bf16[2048,512]{1,0:T(8,128)(2,1)}, u32[]{:S(2)}) %copy-start.8) | copy-done | bytes 2097176
  51.3 0.0 copy-start.10
  51.3 1.0 copy-done.10
  52.3 5.4 %residual.1 = (bf16[2048,512]{1,0:T(8,128)(2,1)S(1)}, bf16[16,16,512]{2,1,0:T(8,128)(2,1)}, bf16[256,512]{1,0:T(8,128)(2,1)S(1)}, f32[8,512]{1,0:T(8,128)S(1)}) custom-call(s32[4,16]{1,0:T(4,128)S(1)} %bitcast.11, s32[4,16]{1,0:T(4,128)S(1)} %bitcast.13, bf16[128,2048]{1,0:T(8,128)(2,1)S(1)} %all_gather.3.mine_ref, bf16[128,2048]{1,0:T(8,128)(2,1)S(1)} %copy-done.10, ...), custom_call_target="tpu_custom_call" | custom-call | flops 1073741824 | bytes 4194304 | tf_op jit(solution)/shard_map/residual/pallas_call | solution.py:115
  57.7 11.7 %all-to-all-start.2 = ((bf16[16,16,512]{2,1,0:T(8,128)(2,1)}), bf16[16,16,512]{2,1,0:T(8,128)(2,1)S(1)}, u32[]{:S(2)}, u32[]{:S(2)}) async-start(bf16[16,16,512]{2,1,0:T(8,128)(2,1)} %get-tuple-element.33), calls=%async_computation.2 | async-start | bytes 524288 | tf_op jit(solution)/shard_map/all_to_all | solution.py:311
  69.4 0.0 copy-start.1
  69.4 0.0 copy-start.3
  69.4 0.0 copy-start.5
  69.4 0.0 copy-start.7
  69.4 1.6 %user_share.1 = (bf16[128,2048]{1,0:T(8,128)(2,1)S(1)}, bf16[128,2048]{1,0:T(8,128)(2,1)}) custom-call(bf16[256,512]{1,0:T(8,128)(2,1)S(1)} %get-tuple-element.25.item_ref, bf16[2048,512]{1,0:T(8,128)(2,1)S(1)} %get-tuple-element.26.scaled_ref), custom_call_target="tpu_custom_call" | custom-call | flops 536870912 | tf_op jit(solution)/shard_map/user_share/pallas_call | solution.py:152
  71.0 2.6 %collective-permute-start.1 = (bf16[128,2048]{1,0:T(8,128)(2,1)}, bf16[128,2048]{1,0:T(8,128)(2,1)S(1)}, u32[]{:S(2)}, u32[]{:S(2)}) collective-permute-start(bf16[128,2048]{1,0:T(8,128)(2,1)} %get-tuple-element.28), channel_id=1, source_target_pairs={{0,1},{1,0},{2,3},{3,2},{4,5},{5,4},{6,7},{7,6},{8,9},{9,8},{10,11... | collective-permute-start | bytes 1572872 | tf_op jit(solution)/shard_map/ppermute | solution.py:316
  73.6 1.7 %collective-permute-done.1 = bf16[128,2048]{1,0:T(8,128)(2,1)S(1)} collective-permute-done((bf16[128,2048]{1,0:T(8,128)(2,1)}, bf16[128,2048]{1,0:T(8,128)(2,1)S(1)}, u32[]{:S(2)}, u32[]{:S(2)}) %collective-permute-start.1) | collective-permute-done | bytes 524320 | tf_op jit(solution)/shard_map/ppermute | solution.py:316
  75.3 0.1 halves.1
  75.4 2.7 %collective-permute-start.2 = (bf16[32,2048]{1,0:T(8,128)(2,1)S(1)}, bf16[32,2048]{1,0:T(8,128)(2,1)S(1)}, u32[]{:S(2)}, u32[]{:S(2)}) collective-permute-start(bf16[32,2048]{1,0:T(8,128)(2,1)S(1)} %get-tuple-element.30), channel_id=1, source_target_pairs={{0,8},{8,16},{16,24},{24,0},{1,9},{9,17},{17,25},{25,1},{2,10},{10... | collective-permute-start | bytes 393224 | tf_op jit(solution)/shard_map/ppermute | solution.py:316
  78.1 4.3 %collective-permute-start.3 = (bf16[32,2048]{1,0:T(8,128)(2,1)S(1)}, bf16[32,2048]{1,0:T(8,128)(2,1)S(1)}, u32[]{:S(2)}, u32[]{:S(2)}) collective-permute-start(bf16[32,2048]{1,0:T(8,128)(2,1)S(1)} %get-tuple-element.31), channel_id=1, source_target_pairs={{0,16},{8,24},{16,0},{24,8},{1,17},{9,25},{17,1},{25,9},{2,18},{10... | collective-permute-start | bytes 393224 | tf_op jit(solution)/shard_map/ppermute | solution.py:316
  82.4 3.0 %collective-permute-start.4 = (bf16[32,2048]{1,0:T(8,128)(2,1)S(1)}, bf16[32,2048]{1,0:T(8,128)(2,1)S(1)}, u32[]{:S(2)}, u32[]{:S(2)}) collective-permute-start(bf16[32,2048]{1,0:T(8,128)(2,1)S(1)} %get-tuple-element.32), channel_id=1, source_target_pairs={{0,24},{8,0},{16,8},{24,16},{1,25},{9,1},{17,9},{25,17},{2,26},{10... | collective-permute-start | bytes 393224 | tf_op jit(solution)/shard_map/ppermute | solution.py:316
  85.5 0.0 collective-permute-done.2.refs_1_
  85.5 1.1 collective-permute-done.3.refs_2_
  86.6 1.9 %collective-permute-done.4.refs_3_ = bf16[32,2048]{1,0:T(8,128)(2,1)S(1)} collective-permute-done((bf16[32,2048]{1,0:T(8,128)(2,1)S(1)}, bf16[32,2048]{1,0:T(8,128)(2,1)S(1)}, u32[]{:S(2)}, u32[]{:S(2)}) %collective-permute-start.4) | collective-permute-done | bytes 131104 | tf_op jit(solution)/shard_map/ppermute | solution.py:316
  88.5 0.7 blocks.1
  89.2 0.0 all-to-all-done.2.arrived_ref
  89.2 3.6 %all-to-all-start.1 = ((bf16[4,8,2048]{2,1,0:T(8,128)(2,1)}), bf16[4,8,2048]{2,1,0:T(8,128)(2,1)S(1)}, u32[]{:S(2)}, u32[]{:S(2)}) async-start(bf16[4,8,2048]{2,1,0:T(8,128)(2,1)} %bitcast.6), calls=%async_computation.1 | async-start | bytes 262144 | tf_op jit(solution)/shard_map/all_to_all | solution.py:311
  92.8 0.0 copy-done.1
  92.8 0.0 copy-done.3
  92.8 0.0 copy-done.5
  92.8 0.0 copy-done.7
  92.8 0.2 item_raw.1
  93.0 4.6 %all-to-all-done.1.arrived_ref = bf16[4,8,2048]{2,1,0:T(8,128)(2,1)S(1)} async-done(((bf16[4,8,2048]{2,1,0:T(8,128)(2,1)}), bf16[4,8,2048]{2,1,0:T(8,128)(2,1)S(1)}, u32[]{:S(2)}, u32[]{:S(2)}) %all-to-all-start.1) | async-done | bytes 131104 | tf_op jit(solution)/shard_map/all_to_all | solution.py:311
  97.6 0.2 user_raw.1
  97.8 14.1 %all_to_all.25.arrived_ref = f32[32,1,128]{2,1,0:T(1,128)S(1)} all-to-all(f32[32,1,128]{2,1,0:T(1,128)S(1)} %get-tuple-element.36), channel_id=1, replica_groups=mesh['row'=16,'col_0'=4,'col_1'=4,'layer'=2] {'col_0','col_1','layer'}, dimensions={0} | all-to-all | bytes 32768 | tf_op jit(solution)/shard_map/all_to_all | solution.py:311
  111.9 22.9 %all_to_all.26.arrived_ref = f32[16,1,128]{2,1,0:T(1,128)S(1)} all-to-all(f32[16,1,128]{2,1,0:T(1,128)S(1)} %packed_again.1), channel_id=1, replica_groups=mesh['row'=16,'col_0'=4,'col_1'=4,'layer'=2] {'row'}, dimensions={0} | all-to-all | bytes 16384 | tf_op jit(solution)/shard_map/all_to_all | solution.py:311
  134.8 0.8 step.1
  135.6 0.6 fusion
  (1 shorter events, 0.0 us)
Async XLA Ops:
  0.6 0.8 copy-start
  1.5 0.8 copy-start.2
  3.0 45.4 %all-to-all-start = ((bf16[16,16,512]{2,1,0:T(8,128)(2,1)}), bf16[16,16,512]{2,1,0:T(8,128)(2,1)S(1)}, u32[]{:S(2)}, u32[]{:S(2)}) async-start(bf16[16,16,512]{2,1,0:T(8,128)(2,1)} %get-tuple-element.24), calls=%async_computation | async-start | bytes 524288 | tf_op jit(solution)/shard_map/all_to_all | solution.py:311
  38.7 8.9 %collective-permute-start = (bf16[128,2048]{1,0:T(8,128)(2,1)S(1)}, bf16[128,2048]{1,0:T(8,128)(2,1)S(1)}, u32[]{:S(2)}, u32[]{:S(2)}) collective-permute-start(bf16[128,2048]{1,0:T(8,128)(2,1)S(1)} %all_gather.3.mine_ref), channel_id=1, source_target_pairs={{0,1},{1,0},{2,3},{3,2},{4,5},{5,4},{6,7},{7,6},{8,9},{9,8},{10,11... | collective-permute-start | bytes 1572872 | tf_op jit(solution)/shard_map/ppermute | solution.py:316
  47.5 0.8 copy-start.9
  48.3 0.7 copy-start.4
  49.0 0.7 copy-start.6
  49.7 1.6 %copy-start.8 = (bf16[2048,512]{1,0:T(8,128)(2,1)S(1)}, bf16[2048,512]{1,0:T(8,128)(2,1)}, u32[]{:S(2)}) copy-start(bf16[2048,512]{1,0:T(8,128)(2,1)} %far_ratings_ref.1) | copy-start | bytes 6291460
  51.3 1.0 copy-start.10
  57.7 31.5 %all-to-all-start.2 = ((bf16[16,16,512]{2,1,0:T(8,128)(2,1)}), bf16[16,16,512]{2,1,0:T(8,128)(2,1)S(1)}, u32[]{:S(2)}, u32[]{:S(2)}) async-start(bf16[16,16,512]{2,1,0:T(8,128)(2,1)} %get-tuple-element.33), calls=%async_computation.2 | async-start | bytes 524288 | tf_op jit(solution)/shard_map/all_to_all | solution.py:311
  69.4 23.4 %copy-start.1 = (f32[8,2048]{1,0:T(8,128)S(1)}, f32[8,2048]{1,0:T(8,128)}, u32[]{:S(2)}) copy-start(f32[8,2048]{1,0:T(8,128)} %user_ref.5) | copy-start | bytes 196612
  69.4 23.4 %copy-start.3 = (f32[16,512]{1,0:T(8,128)S(1)}, f32[16,512]{1,0:T(8,128)}, u32[]{:S(2)}) copy-start(f32[16,512]{1,0:T(8,128)} %item_ref.5) | copy-start | bytes 98308
  69.4 23.4 %copy-start.5 = (s32[16,4]{0,1:T(4,128)S(1)}, s32[16,4]{0,1:T(4,128)}, u32[]{:S(2)}) copy-start(s32[16,4]{0,1:T(4,128)} %param.6) | copy-start | bytes 772
  69.4 23.4 %copy-start.7 = (s32[16,4]{0,1:T(4,128)S(1)}, s32[16,4]{0,1:T(4,128)}, u32[]{:S(2)}) copy-start(s32[16,4]{0,1:T(4,128)} %param.7) | copy-start | bytes 772
  71.0 4.3 %collective-permute-start.1 = (bf16[128,2048]{1,0:T(8,128)(2,1)}, bf16[128,2048]{1,0:T(8,128)(2,1)S(1)}, u32[]{:S(2)}, u32[]{:S(2)}) collective-permute-start(bf16[128,2048]{1,0:T(8,128)(2,1)} %get-tuple-element.28), channel_id=1, source_target_pairs={{0,1},{1,0},{2,3},{3,2},{4,5},{5,4},{6,7},{7,6},{8,9},{9,8},{10,11... | collective-permute-start | bytes 1572872 | tf_op jit(solution)/shard_map/ppermute | solution.py:316
  75.4 10.1 %collective-permute-start.2 = (bf16[32,2048]{1,0:T(8,128)(2,1)S(1)}, bf16[32,2048]{1,0:T(8,128)(2,1)S(1)}, u32[]{:S(2)}, u32[]{:S(2)}) collective-permute-start(bf16[32,2048]{1,0:T(8,128)(2,1)S(1)} %get-tuple-element.30), channel_id=1, source_target_pairs={{0,8},{8,16},{16,24},{24,0},{1,9},{9,17},{17,25},{25,1},{2,10},{10... | collective-permute-start | bytes 393224 | tf_op jit(solution)/shard_map/ppermute | solution.py:316
  78.1 8.4 %collective-permute-start.3 = (bf16[32,2048]{1,0:T(8,128)(2,1)S(1)}, bf16[32,2048]{1,0:T(8,128)(2,1)S(1)}, u32[]{:S(2)}, u32[]{:S(2)}) collective-permute-start(bf16[32,2048]{1,0:T(8,128)(2,1)S(1)} %get-tuple-element.31), channel_id=1, source_target_pairs={{0,16},{8,24},{16,0},{24,8},{1,17},{9,25},{17,1},{25,9},{2,18},{10... | collective-permute-start | bytes 393224 | tf_op jit(solution)/shard_map/ppermute | solution.py:316
  82.4 6.0 %collective-permute-start.4 = (bf16[32,2048]{1,0:T(8,128)(2,1)S(1)}, bf16[32,2048]{1,0:T(8,128)(2,1)S(1)}, u32[]{:S(2)}, u32[]{:S(2)}) collective-permute-start(bf16[32,2048]{1,0:T(8,128)(2,1)S(1)} %get-tuple-element.32), channel_id=1, source_target_pairs={{0,24},{8,0},{16,8},{24,16},{1,25},{9,1},{17,9},{25,17},{2,26},{10... | collective-permute-start | bytes 393224 | tf_op jit(solution)/shard_map/ppermute | solution.py:316
  89.2 8.5 %all-to-all-start.1 = ((bf16[4,8,2048]{2,1,0:T(8,128)(2,1)}), bf16[4,8,2048]{2,1,0:T(8,128)(2,1)S(1)}, u32[]{:S(2)}, u32[]{:S(2)}) async-start(bf16[4,8,2048]{2,1,0:T(8,128)(2,1)} %bitcast.6), calls=%async_computation.1 | async-start | bytes 262144 | tf_op jit(solution)/shard_map/all_to_all | solution.py:311

commit v4 on v3

v4 whole, which is shorter than its diff:
```python
import jax
import jax.numpy as jnp
from jax import lax
from jax.experimental import pallas as pl
from jax.experimental.pallas import tpu as pltpu
from jax.sharding import Mesh
from jax.sharding import PartitionSpec as P

TILE = 128
LANES = 128
STRIPE = 512
COL_LAYER = ("col_0", "col_1", "layer")
VMEM = pl.BlockSpec(memory_space=pltpu.VMEM)
SMEM = pl.BlockSpec(memory_space=pltpu.SMEM)
FAR = pl.BlockSpec(memory_space=pltpu.HBM)
GRANT = pltpu.CompilerParams(vmem_limit_bytes=16 * 2**20)

epsilon = 1e-12
trust_ratio = 0.2


def lower_body(user_ref, blocks_ref):
    user = user_ref[...].astype(jnp.bfloat16)
    blocks_ref[...] = jnp.broadcast_to(user[None], blocks_ref.shape)


def lowered_for_all(factor, devices):
    return pl.pallas_call(
        lower_body,
        in_specs=[VMEM],
        out_specs=VMEM,
        out_shape=jax.ShapeDtypeStruct((devices, *factor.shape), jnp.bfloat16),
        compiler_params=GRANT,
        name="lower",
    )(factor)


def residual_body(
    far_mask_ref, far_counts_ref, far_user_ref, far_item_ref, far_ratings_ref,
    scaled_ref, item_share_ref, error_ref,
    mask_ref, counts_ref, user_ref, item_ref, ratings_ref, total_ref, sems, ratings_sems,
):
    columns = ratings_ref.shape[1]
    starts = range(0, ratings_ref.shape[0], STRIPE)
    stripes = [pl.ds(start, STRIPE) for start in starts]
    copies = [
        pltpu.make_async_copy(far, near, sems.at[at])
        for at, (far, near) in enumerate(
            (
                (far_user_ref, user_ref),
                (far_item_ref, item_ref),
                (far_mask_ref, mask_ref),
                (far_counts_ref, counts_ref),
            )
        )
    ]
    ratings_copies = [
        pltpu.make_async_copy(far_ratings_ref.at[stripe], ratings_ref.at[stripe], ratings_sems.at[at])
        for at, stripe in enumerate(stripes)
    ]
    for copy in copies + ratings_copies:
        copy.start()
    for copy in copies:
        copy.wait()
    item = item_ref[...]
    side = (TILE, TILE)
    position = lax.broadcasted_iota(jnp.int32, side, 0) * TILE + lax.broadcasted_iota(jnp.int32, side, 1)

    def predicted_of(at):
        user = user_ref[:, stripes[at]]
        return lax.dot_general(user, item, (((0,), (0,)), ((), ())), preferred_element_type=jnp.float32)

    def add_share(at):
        share = jnp.dot(user_ref[:, stripes[at]], scaled_ref[stripes[at]], preferred_element_type=jnp.float32)
        if at > 0:
            share = share + total_ref[...]
        if at + 1 < len(stripes):
            total_ref[...] = share
        else:
            item_share_ref[...] = share.astype(jnp.bfloat16).reshape(item_share_ref.shape)

    predicted = predicted_of(0)
    errors = [jnp.zeros((8, TILE), jnp.float32)] * (columns // TILE)
    for at, start in enumerate(starts):
        ratings_copies[at].wait()
        following = predicted_of(at + 1) if at + 1 < len(stripes) else None
        for row in range(0, STRIPE, TILE):
            for column in range(0, columns, TILE):
                tile_at = (column // TILE, (start + row) // TILE)
                limit = jnp.where(mask_ref[tile_at] == 1, counts_ref[tile_at], 0)
                rows, cols = pl.ds(start + row, TILE), pl.ds(column, TILE)
                rating = ratings_ref[rows, cols].astype(jnp.float32)
                difference = predicted[row : row + TILE, column : column + TILE] - rating
                residual = jnp.where(position < limit, difference, 0.0)
                scaled_ref[rows, cols] = residual.astype(jnp.bfloat16)
                error = (residual * residual).reshape(TILE // 8, 8, TILE).sum(axis=0)
                errors[column // TILE] = errors[column // TILE] + error
        if at > 0:
            add_share(at - 1)
        predicted = following
    add_share(len(stripes) - 1)
    error_ref[...] = jnp.concatenate(errors, axis=1)


def residual_of(mask, counts, user, item, ratings, devices):
    rank, columns = item.shape
    flops = 4 * rank * ratings.size
    return pl.pallas_call(
        residual_body,
        in_specs=[FAR] * 5,
        out_specs=[VMEM] * 3,
        out_shape=[
            jax.ShapeDtypeStruct(ratings.shape, jnp.bfloat16),
            jax.ShapeDtypeStruct((devices, rank // devices, columns), jnp.bfloat16),
            jax.ShapeDtypeStruct((8, columns), jnp.float32),
        ],
        scratch_shapes=[
            pltpu.SMEM(mask.shape, jnp.int32),
            pltpu.SMEM(counts.shape, jnp.int32),
            pltpu.VMEM(user.shape, jnp.bfloat16),
            pltpu.VMEM(item.shape, jnp.bfloat16),
            pltpu.VMEM(ratings.shape, jnp.bfloat16),
            pltpu.VMEM((rank, columns), jnp.float32),
            pltpu.SemaphoreType.DMA((4,)),
            pltpu.SemaphoreType.DMA((ratings.shape[0] // STRIPE,)),
        ],
        cost_estimate=pl.CostEstimate(flops=flops, bytes_accessed=4 * ratings.size, transcendentals=0),
        compiler_params=GRANT,
        name="residual",
    )(mask, counts, user, item, ratings)


def user_share_body(layer_ref, item_ref, scaled_ref, mine_ref, other_ref):
    chips, height, _ = mine_ref.shape
    item = item_ref[...]
    first = layer_ref[0] == 0
    for start in range(0, scaled_ref.shape[0], STRIPE):
        stripe = pl.ds(start, STRIPE)
        share = lax.dot_general(item, scaled_ref[stripe], (((1,), (1,)), ((), ())), preferred_element_type=jnp.float32)
        share = share.reshape(chips, 2, height, STRIPE)
        even, odd = share[:, 0], share[:, 1]
        mine_ref[:, :, stripe] = jnp.where(first, even, odd).astype(jnp.bfloat16)
        other_ref[:, :, stripe] = jnp.where(first, odd, even).astype(jnp.bfloat16)


def user_share_of(layer, item, scaled, height):
    shape = jax.ShapeDtypeStruct((item.shape[0] // height // 2, height, scaled.shape[0]), jnp.bfloat16)
    return pl.pallas_call(
        user_share_body,
        in_specs=[SMEM, VMEM, VMEM],
        out_specs=[VMEM, VMEM],
        out_shape=[shape, shape],
        cost_estimate=pl.CostEstimate(flops=2 * item.shape[0] * scaled.size, bytes_accessed=0, transcendentals=0),
        compiler_params=GRANT,
        name="user_share",
    )(layer, item, scaled)


def halves_body(mine_ref, arrived_ref, total_ref):
    total_ref[...] = (mine_ref[...].astype(jnp.float32) + arrived_ref[...].astype(jnp.float32)).astype(jnp.bfloat16)


def halves_summed(mine, arrived):
    return pl.pallas_call(
        halves_body,
        in_specs=[VMEM, VMEM],
        out_specs=VMEM,
        out_shape=jax.ShapeDtypeStruct(mine.shape, jnp.bfloat16),
        compiler_params=GRANT,
        name="halves",
    )(mine, arrived)


def summed(blocks_ref):
    total = blocks_ref[0].astype(jnp.float32)
    for i in range(1, blocks_ref.shape[0]):
        total = total + blocks_ref[i].astype(jnp.float32)
    return total


def item_raw_body(mask_ref, counts_ref, arrived_ref, user_ref, item_ref, error_ref, raw_ref, sums_ref):
    raw = summed(arrived_ref)
    raw_ref[...] = raw
    user, item = user_ref[...], item_ref[...]
    lane = lax.broadcasted_iota(jnp.int32, sums_ref.shape, 1)
    sums = jnp.zeros(sums_ref.shape, jnp.float32)
    for at, value in enumerate(
        (
            jnp.sum((mask_ref[...] * counts_ref[...]).astype(jnp.float32)),
            jnp.sum(user * user) + jnp.sum(item * item),
            jnp.sum(error_ref[...]),
            jnp.sum(raw * raw),
        )
    ):
        sums = jnp.where(lane == at, value, sums)
    sums_ref[...] = sums


def item_raw_of(mask, counts, arrived, user_factor, item_factor, error):
    return pl.pallas_call(
        item_raw_body,
        in_specs=[VMEM] * 6,
        out_specs=[VMEM, VMEM],
        out_shape=[
            jax.ShapeDtypeStruct(arrived.shape[1:], jnp.float32),
            jax.ShapeDtypeStruct((1, LANES), jnp.float32),
        ],
        compiler_params=GRANT,
        name="item_raw",
    )(mask, counts, arrived, user_factor, item_factor, error)


def user_raw_body(arrived_ref, sums_ref, raw_ref, packed_ref):
    raw = summed(arrived_ref)
    raw_ref[...] = raw
    lane = lax.broadcasted_iota(jnp.int32, sums_ref.shape, 1)
    sums = sums_ref[...] + jnp.where(lane == 3, jnp.sum(raw * raw), 0.0)
    packed_ref[...] = jnp.broadcast_to(sums[None], packed_ref.shape)


def user_raw_of(arrived, sums, devices):
    return pl.pallas_call(
        user_raw_body,
        in_specs=[VMEM, VMEM],
        out_specs=[VMEM, VMEM],
        out_shape=[
            jax.ShapeDtypeStruct(arrived.shape[1:], jnp.float32),
            jax.ShapeDtypeStruct((devices, *sums.shape), jnp.float32),
        ],
        compiler_params=GRANT,
        name="user_raw",
    )(arrived, sums)


def packed_again_body(arrived_ref, packed_ref):
    packed_ref[...] = jnp.broadcast_to(summed(arrived_ref)[None], packed_ref.shape)


def packed_again(arrived, devices):
    return pl.pallas_call(
        packed_again_body,
        in_specs=[VMEM],
        out_specs=VMEM,
        out_shape=jax.ShapeDtypeStruct((devices, *arrived.shape[1:]), jnp.float32),
        compiler_params=GRANT,
        name="packed_again",
    )(arrived)


def step_body(arrived_ref, user_ref, item_ref, raw_user_ref, raw_item_ref, new_user_ref, new_item_ref, ends_ref):
    sums = summed(arrived_ref)
    lane = lax.broadcasted_iota(jnp.int32, sums.shape, 1)

    def lane_at(at):
        return jnp.sum(jnp.where(lane == at, sums, 0.0), axis=1, keepdims=True)

    observed_total = jnp.maximum(lane_at(0), 1.0)
    scale = 2.0 / observed_total
    grad_norm = scale * jnp.sqrt(lane_at(3) + epsilon)
    step_size = trust_ratio * jnp.sqrt(lane_at(1) + epsilon) / grad_norm * scale
    new_user_ref[...] = user_ref[...] - step_size * raw_user_ref[...]
    new_item_ref[...] = item_ref[...] - step_size * raw_item_ref[...]
    ends_ref[...] = jnp.where(lane == 0, lane_at(2) / observed_total, grad_norm)


def stepped(arrived, user_factor, item_factor, raw_user, raw_item):
    return pl.pallas_call(
        step_body,
        in_specs=[VMEM] * 5,
        out_specs=[VMEM] * 3,
        out_shape=[
            jax.ShapeDtypeStruct(user_factor.shape, jnp.float32),
            jax.ShapeDtypeStruct(item_factor.shape, jnp.float32),
            jax.ShapeDtypeStruct(arrived.shape[1:], jnp.float32),
        ],
        compiler_params=GRANT,
        name="step",
    )(arrived, user_factor, item_factor, raw_user, raw_item)


def exchanged(blocks, axis):
    return lax.all_to_all(blocks, axis, 0, 0, tiled=True)


def shifted(array, axis, by):
    count = lax.axis_size(axis)
    return lax.ppermute(array, axis, [(i, (i + by) % count) for i in range(count)])


def body(ratings, tile_mask, tile_counts, user_factor, item_factor):
    rows, height = lax.axis_size("row"), user_factor.shape[0]
    layer = lax.axis_index("layer").astype(jnp.int32)[None]
    mask, counts = tile_mask.T, tile_counts.T
    user = exchanged(lowered_for_all(user_factor, lax.axis_size(COL_LAYER)), COL_LAYER)
    user = user.reshape(-1, user_factor.shape[1])
    item = lax.all_gather(item_factor.astype(jnp.bfloat16), "row", axis=0, tiled=True)
    scaled, item_share, error = residual_of(mask, counts, user, item, ratings, rows)
    item_arrived = exchanged(item_share, "row")
    my_share, other_share = user_share_of(layer, item, scaled, height)
    partner_share = shifted(other_share, "layer", 1)
    halves = halves_summed(my_share, partner_share)
    user_arrived = exchanged(halves, ("col_0", "col_1"))
    raw_item, sums = item_raw_of(mask, counts, item_arrived, user_factor, item_factor, error)
    raw_user, packed = user_raw_of(user_arrived, sums, lax.axis_size(COL_LAYER))
    packed = exchanged(packed, COL_LAYER)
    packed = packed_again(packed, rows)
    packed = exchanged(packed, "row")
    new_user, new_item, ends = stepped(packed, user_factor, item_factor, raw_user, raw_item)
    return (new_user, new_item, ends[0, 0], ends[0, 1])


def solution(mesh):
    finer = Mesh(
        mesh.devices.reshape(mesh.shape["row"], 4, 4, mesh.shape["layer"]),
        ("row", "col_0", "col_1", "layer"),
    )
    return jax.shard_map(
        body,
        mesh=finer,
        in_specs=(
            P("row", COL_LAYER),
            P("row", COL_LAYER),
            P("row", COL_LAYER),
            P(COL_LAYER, "row"),
            P("row", COL_LAYER),
        ),
        out_specs=(P(COL_LAYER, "row"), P("row", COL_LAYER), P(), P()),
        check_vma=False,
    )
```

time: 137 us -> 121 us (0.88)
  starting transfers between devices: 51 us -> 32 us
  blocking collectives: 56.9 us -> 64.7 us
  local copies, waits for them, and re-layouts: 7 us -> 3.71 us
  Pallas kernels: 9.62 us -> 7.41 us
    ppermute x5 -> x1, starting transfers between devices: 20 us -> 8.19 us  [shifted(): lax.ppermute(array, axis, [(i, (i + by) % count) for i in range(count)])]
    all_gather x1, blocking collectives: 19.9 us -> 28.6 us  [body(): lax.all_gather(item_factor.astype(jnp.bfloat16), 'row', axis=0, tiled=True)]
    all_to_all x3, starting transfers between devices: 31 us -> 23.8 us  [exchanged(): return lax.all_to_all(blocks, axis, 0, 0, tiled=True)]
    all_to_all x3, waiting for transfers between devices: 4.63 us -> 10.2 us  [exchanged(): return lax.all_to_all(blocks, axis, 0, 0, tiled=True)]
    ppermute x5 -> x1, waiting for transfers between devices: 6.19 us -> 1.51 us  [shifted(): lax.ppermute(array, axis, [(i, (i + by) % count) for i in range(count)])]
    unnamed x22 -> x14, local copies, waits for them, and re-layouts: 6.42 us -> 3.13 us
    pallas_call x6 -> x5, Pallas kernels: 8.67 us -> 6.4 us  [the longest x1 3.47 us: residual_of(): pl.pallas_call(residual_body, in_specs=[FAR] * 5, out_specs=[VMEM] * 3, o...]
  transfers between devices with their start and end apart: 8 -> 4, of which waited for: 5 -> 3; matrix products, arithmetic and copies ran while one was open for 0% -> 0% of each run, Pallas kernels for 2% -> 2%
where the time goes in v4:
time: 121 us; the launch traced here: 120 us
  blocking collectives  64.7 us (53%)
  starting transfers between devices  32 us (26%)
  waiting for transfers between devices  11.7 us (10%)
  Pallas kernels  7.41 us (6%)
  local copies, waits for them, and re-layouts  3.71 us (3%)
    all_to_all x2, blocking collectives, exchanged(): return lax.all_to_all(blocks, axis, 0, 0, tiled=True)  36.1 us
    all_gather x1, blocking collectives, body(): lax.all_gather(item_factor.astype(jnp.bfloat16), 'row', axis=0, tiled=True)  28.6 us
    all_to_all x3, starting transfers between devices, exchanged(): return lax.all_to_all(blocks, axis, 0, 0, tiled=True)  23.8 us
    all_to_all x3, waiting for transfers between devices, exchanged(): return lax.all_to_all(blocks, axis, 0, 0, tiled=True)  10.2 us
    ppermute x1, starting transfers between devices, shifted(): lax.ppermute(array, axis, [(i, (i + by) % count) for i in range(count)])  8.19 us
    pallas_call x1, Pallas kernels, residual_of(): pl.pallas_call(residual_body, in_specs=[FAR] * 5, out_specs=[VMEM] * 3, o...  3.47 us
    unnamed x14, local copies, waits for them, and re-layouts  3.13 us
  transfers between devices with their start and end apart: 4, of which 3 were waited for; matrix products, arithmetic and copies ran while one was open for 0% of the time, Pallas kernels for 2%

profile of v4, /device:TPU:1, one launch (start us, length us, event | category | flops | bytes accessed | tf_op | source)
XLA Modules:
  0.0 120.3 jit_solution(14507252790831366506)
XLA Ops:
  0.6 0.0 copy-start
  0.6 0.8 copy-done
  1.5 0.0 copy-start.2
  1.5 0.0 copy-start.4
  1.5 0.0 copy-start.5
  1.5 1.1 lower.1
  2.6 10.4 %all-to-all-start = ((bf16[32,8,2048]{2,1,0:T(8,128)(2,1)}), bf16[32,8,2048]{2,1,0:T(8,128)(2,1)S(1)}, u32[]{:S(2)}, u32[]{:S(2)}) async-start(bf16[32,8,2048]{2,1,0:T(8,128)(2,1)} %lower.1), calls=%async_computation | async-start | bytes 2097152 | tf_op jit(solution)/shard_map/all_to_all | solution.py:282
  13.0 0.0 copy-done.2
  13.0 28.6 %all_gather.3.far_item_ref.item_ref = bf16[256,512]{1,0:T(8,128)(2,1)S(1)} all-gather(bf16[16,512]{1,0:T(8,128)(2,1)S(1)} %convert_element_type.3), channel_id=1, replica_groups=mesh['row'=16,'col_0'=4,'col_1'=4,'layer'=2] {'row'}, dimensions={0}, use_global_device_ids=true | all-gather | bytes 278528 | tf_op jit(solution)/shard_map/all_gather | solution.py:296
  41.6 0.0 all-to-all-done
  41.6 0.0 copy-done.4
  41.6 0.0 copy-done.5
  41.6 0.0 copy-start.6
  41.6 1.6 %copy-done.6 = bf16[2048,512]{1,0:T(8,128)(2,1)S(1)} copy-done((bf16[2048,512]{1,0:T(8,128)(2,1)S(1)}, bf16[2048,512]{1,0:T(8,128)(2,1)}, u32[]{:S(2)}) %copy-start.6) | copy-done | bytes 2097176
  43.2 3.5 %residual.1 = (bf16[2048,512]{1,0:T(8,128)(2,1)S(1)}, bf16[16,16,512]{2,1,0:T(8,128)(2,1)S(1)}, f32[8,512]{1,0:T(8,128)S(1)}) custom-call(s32[4,16]{1,0:T(4,128)S(1)} %bitcast.7, s32[4,16]{1,0:T(4,128)S(1)} %bitcast.9, bf16[256,2048]{1,0:T(8,128)(2,1)S(1)} %bitcast.6, bf16[256,512]{1,0:T(8,128)(2,1)S(1)} %all_gather.3.far_item_ref.item_ref, ...), custom_call_target="tpu_custom_call" | custom-call | flops 1073741824 | bytes 4194304 | tf_op jit(solution)/shard_map/residual/pallas_call | solution.py:108
  46.7 0.0 copy-start.3
  46.7 0.7 copy-done.3
  47.4 7.0 %all-to-all-start.2 = ((bf16[16,16,512]{2,1,0:T(8,128)(2,1)}), bf16[16,16,512]{2,1,0:T(8,128)(2,1)S(1)}, u32[]{:S(2)}, u32[]{:S(2)}) async-start(bf16[16,16,512]{2,1,0:T(8,128)(2,1)} %copy-done.3), calls=%async_computation.2 | async-start | bytes 524288 | tf_op jit(solution)/shard_map/all_to_all | solution.py:282
  54.4 0.0 copy-start.1
  54.5 0.7 user_share.1
  55.2 8.2 %collective-permute-start = (bf16[16,8,2048]{2,1,0:T(8,128)(2,1)S(1)}, bf16[16,8,2048]{2,1,0:T(8,128)(2,1)S(1)}, u32[]{:S(2)}, u32[]{:S(2)}) collective-permute-start(bf16[16,8,2048]{2,1,0:T(8,128)(2,1)S(1)} %get-tuple-element.18), channel_id=1, source_target_pairs={{0,1},{1,0},{2,3},{3,2},{4,5},{5,4},{6,7},{7,6},{8,9},{9,8},{10,11... | collective-permute-start | bytes 1572872 | tf_op jit(solution)/shard_map/ppermute | solution.py:287
  63.4 1.5 %collective-permute-done.arrived_ref = bf16[16,8,2048]{2,1,0:T(8,128)(2,1)S(1)} collective-permute-done((bf16[16,8,2048]{2,1,0:T(8,128)(2,1)S(1)}, bf16[16,8,2048]{2,1,0:T(8,128)(2,1)S(1)}, u32[]{:S(2)}, u32[]{:S(2)}) %collective-permute-start) | collective-permute-done | bytes 524320 | tf_op jit(solution)/shard_map/ppermute | solution.py:287
  64.9 0.9 halves.1
  65.8 1.4 %all-to-all-done.2.arrived_ref = bf16[16,16,512]{2,1,0:T(8,128)(2,1)S(1)} async-done(((bf16[16,16,512]{2,1,0:T(8,128)(2,1)}), bf16[16,16,512]{2,1,0:T(8,128)(2,1)S(1)}, u32[]{:S(2)}, u32[]{:S(2)}) %all-to-all-start.2) | async-done | bytes 262176 | tf_op jit(solution)/shard_map/all_to_all | solution.py:282
  67.3 6.4 %all-to-all-start.1 = ((bf16[16,8,2048]{2,1,0:T(8,128)(2,1)}), bf16[16,8,2048]{2,1,0:T(8,128)(2,1)S(1)}, u32[]{:S(2)}, u32[]{:S(2)}) async-start(bf16[16,8,2048]{2,1,0:T(8,128)(2,1)} %halves.1), calls=%async_computation.1 | async-start | bytes 1048576 | tf_op jit(solution)/shard_map/all_to_all | solution.py:282
  73.7 0.0 copy-done.1
  73.7 0.2 item_raw.1
  73.8 8.8 %all-to-all-done.1.arrived_ref = bf16[16,8,2048]{2,1,0:T(8,128)(2,1)S(1)} async-done(((bf16[16,8,2048]{2,1,0:T(8,128)(2,1)}), bf16[16,8,2048]{2,1,0:T(8,128)(2,1)S(1)}, u32[]{:S(2)}, u32[]{:S(2)}) %all-to-all-start.1) | async-done | bytes 524320 | tf_op jit(solution)/shard_map/all_to_all | solution.py:282
  82.6 0.2 user_raw.1
  82.9 19.4 %all_to_all.25.arrived_ref = f32[32,1,128]{2,1,0:T(1,128)S(1)} all-to-all(f32[32,1,128]{2,1,0:T(1,128)S(1)} %get-tuple-element.22), channel_id=1, replica_groups=mesh['row'=16,'col_0'=4,'col_1'=4,'layer'=2] {'col_0','col_1','layer'}, dimensions={0} | all-to-all | bytes 32768 | tf_op jit(solution)/shard_map/all_to_all | solution.py:282
  102.3 16.7 %all_to_all.26.arrived_ref = f32[16,1,128]{2,1,0:T(1,128)S(1)} all-to-all(f32[16,1,128]{2,1,0:T(1,128)S(1)} %packed_again.1), channel_id=1, replica_groups=mesh['row'=16,'col_0'=4,'col_1'=4,'layer'=2] {'row'}, dimensions={0} | all-to-all | bytes 16384 | tf_op jit(solution)/shard_map/all_to_all | solution.py:282
  119.0 0.8 step.1
  119.7 0.6 fusion
  (2 shorter events, 0.0 us)
Async XLA Ops:
  0.6 0.8 copy-start
  1.5 11.5 %copy-start.2 = (f32[16,512]{1,0:T(8,128)S(1)}, f32[16,512]{1,0:T(8,128)}, u32[]{:S(2)}) copy-start(f32[16,512]{1,0:T(8,128)} %item_ref.3) | copy-start | bytes 98308
  1.5 40.2 %copy-start.4 = (s32[16,4]{0,1:T(4,128)S(1)}, s32[16,4]{0,1:T(4,128)}, u32[]{:S(2)}) copy-start(s32[16,4]{0,1:T(4,128)} %param.6) | copy-start | bytes 772
  1.5 40.2 %copy-start.5 = (s32[16,4]{0,1:T(4,128)S(1)}, s32[16,4]{0,1:T(4,128)}, u32[]{:S(2)}) copy-start(s32[16,4]{0,1:T(4,128)} %param.7) | copy-start | bytes 772
  2.6 39.0 %all-to-all-start = ((bf16[32,8,2048]{2,1,0:T(8,128)(2,1)}), bf16[32,8,2048]{2,1,0:T(8,128)(2,1)S(1)}, u32[]{:S(2)}, u32[]{:S(2)}) async-start(bf16[32,8,2048]{2,1,0:T(8,128)(2,1)} %lower.1), calls=%async_computation | async-start | bytes 2097152 | tf_op jit(solution)/shard_map/all_to_all | solution.py:282
  41.6 1.6 %copy-start.6 = (bf16[2048,512]{1,0:T(8,128)(2,1)S(1)}, bf16[2048,512]{1,0:T(8,128)(2,1)}, u32[]{:S(2)}) copy-start(bf16[2048,512]{1,0:T(8,128)(2,1)} %far_ratings_ref.1) | copy-start | bytes 6291460
  46.7 0.7 copy-start.3
  47.4 19.9 %all-to-all-start.2 = ((bf16[16,16,512]{2,1,0:T(8,128)(2,1)}), bf16[16,16,512]{2,1,0:T(8,128)(2,1)S(1)}, u32[]{:S(2)}, u32[]{:S(2)}) async-start(bf16[16,16,512]{2,1,0:T(8,128)(2,1)} %copy-done.3), calls=%async_computation.2 | async-start | bytes 524288 | tf_op jit(solution)/shard_map/all_to_all | solution.py:282
  54.4 19.2 %copy-start.1 = (f32[8,2048]{1,0:T(8,128)S(1)}, f32[8,2048]{1,0:T(8,128)}, u32[]{:S(2)}) copy-start(f32[8,2048]{1,0:T(8,128)} %user_ref.5) | copy-start | bytes 196612
  55.2 9.7 %collective-permute-start = (bf16[16,8,2048]{2,1,0:T(8,128)(2,1)S(1)}, bf16[16,8,2048]{2,1,0:T(8,128)(2,1)S(1)}, u32[]{:S(2)}, u32[]{:S(2)}) collective-permute-start(bf16[16,8,2048]{2,1,0:T(8,128)(2,1)S(1)} %get-tuple-element.18), channel_id=1, source_target_pairs={{0,1},{1,0},{2,3},{3,2},{4,5},{5,4},{6,7},{7,6},{8,9},{9,8},{10,11... | collective-permute-start | bytes 1572872 | tf_op jit(solution)/shard_map/ppermute | solution.py:287
  67.3 15.4 %all-to-all-start.1 = ((bf16[16,8,2048]{2,1,0:T(8,128)(2,1)}), bf16[16,8,2048]{2,1,0:T(8,128)(2,1)S(1)}, u32[]{:S(2)}, u32[]{:S(2)}) async-start(bf16[16,8,2048]{2,1,0:T(8,128)(2,1)} %halves.1), calls=%async_computation.1 | async-start | bytes 1048576 | tf_op jit(solution)/shard_map/all_to_all | solution.py:282
